TPU v7x, 256 devices: a 8x8x2 block of a 8x8x16 slice. The times are simulated.
256 devices in a mesh: pop: 2 (over z), dp: 2 (over core), tensor: 64 (over y, x).
Axes of the slice: x: 8, y: 8, z: 2, core: 2. Of those that a mesh axis runs over, the one named last changes fastest.
The devices are a block of a 8x8x16 slice.
Arguments:
- tokens: bfloat16 [1024, 16384], P(('pop', 'dp'), 'tensor'), parts along dimension 0, may hold values from -6 to 6
- weight: bfloat16 [16384, 26624], P('dp', 'tensor'), may hold values from -0.046875 to 0.046875
- adapter_in: bfloat16 [8, 16384, 64], P(('pop', 'dp'), 'tensor'), parts along dimension 0, may hold values from -0.046875 to 0.046875
- adapter_out: bfloat16 [8, 64, 26624], P(('pop', 'dp'), None, 'tensor'), parts along dimension 0, may hold values from -0.375 to 0.375
- cotangent: bfloat16 [1024, 26624], P(('pop', 'dp'), 'tensor'), parts along dimension 0, may hold values from -0.59765625 to 0.59765625
- member_blocks: int32 [8], P('pop'), parts along dimension 0, may hold values from 0 to 3, as said below
- block_live: int32 [8], P(('pop', 'dp')), parts along dimension 0, may hold values from 1 to 128, as said below
Outputs:
- hidden: bfloat16 [1024, 26624], P(('pop', 'dp'), 'tensor'), parts along dimension 0
- input_gradient: bfloat16 [1024, 16384], P(('pop', 'dp'), 'tensor'), parts along dimension 0
- down_factor_gradient: float32 [8, 16384, 64], P(('pop', 'dp'), 'tensor'), parts along dimension 0
- up_factor_gradient: float32 [8, 64, 26624], P(('pop', 'dp'), None, 'tensor'), parts along dimension 0
There are 2 independent parts, one for each index of `pop`. A program takes and returns all parts, laid end to end along the dimension named above; an argument that names none is the same for every part. Nothing has to cross between parts.
Inputs may be any that keep to these rules, and one draw needn't show every extreme that they name: `member_blocks`: the number of 128-token blocks of each member; the counts sum to 4 and the blocks come in order of member. `block_live`: the live tokens stand at the start of each block; every block but the last one of its member is full.
All inputs are finite; a program needn't handle non-finite values.
Results may differ from a plain program's by a relative error of at most 0.003.
Values may be sent and summed in bfloat16 or wider, within the bound.
No kernel may reach another device: no remote copies, remote signals or barrier semaphores. Data moves between devices by JAX's collectives and lax.ppermute only.
A program may use at most 128 MiB of HBM per device.

v0:
```python
import functools
import math

import jax
import jax.numpy as jnp
from jax import lax
from jax.experimental import pallas as pl
from jax.experimental.pallas import tpu as pltpu
from jax.sharding import Mesh
from jax.sharding import PartitionSpec as P

MEMBERS = 4
BLOCK = 128
TENSOR = ("ty", "tx")
GROUP = ("dp", "ty", "tx")
EXTRA = 16
TOP = 32767.0


adapter_scale = 0.5


def ring_pairs(side, step, bulk):
    pairs = []
    for c in range(2):
        for y in range(side):
            for x in range(side):
                along_y = (c == 0) == bulk
                to_y = (y + step) % side if along_y else y
                to_x = x if along_y else (x + step) % side
                pairs.append(
                    ((c * side + y) * side + x, (c * side + to_y) * side + to_x)
                )
    return pairs


def send(x, side, step, bulk):
    return lax.ppermute(x, GROUP, ring_pairs(side, step, bulk))


def swap(x):
    return lax.ppermute(x, "dp", [(0, 1), (1, 0)])


def vmem(x):
    return pltpu.with_memory_space_constraint(x, pltpu.VMEM)


HBM = pl.BlockSpec(memory_space=pltpu.HBM)
ALL_VMEM = pl.BlockSpec(memory_space=pltpu.VMEM)
PARAMS = pltpu.CompilerParams(vmem_limit_bytes=10 << 20)


def ring_place():
    c, y, x = (lax.axis_index(a).astype(jnp.int32) for a in GROUP)
    return c, jnp.where(c == 0, y, x), jnp.where(c == 0, x, y)


def start_weights(weights, buf, sem, side, slot, d, first, count):
    own, other = weights
    n = buf.shape[2]
    here = own.shape[1] // n
    c, p, q = ring_place()
    chunk = lax.rem(p + (d + side), side)

    def begin(k, _):
        piece = lax.rem(q + (side - first) - k, side)
        t = jnp.where(c == 0, side * chunk + piece, side * piece + chunk)
        half = (t >= here).astype(jnp.int32)
        at = pl.ds(pl.multiple_of((t - half * here) * n, n), n)
        to = slot + k

        @pl.when(half == c)
        def _():
            pltpu.make_async_copy(own.at[:, at], buf.at[to], sem.at[to]).start()

        @pl.when(half != c)
        def _():
            pltpu.make_async_copy(other.at[:, at], buf.at[to], sem.at[to]).start()

        return 0

    lax.fori_loop(0, count, begin, 0)


def wait_weight(weights, buf, sem, slot):
    n = buf.shape[2]
    pltpu.make_async_copy(weights[0].at[:, pl.ds(0, n)], buf.at[slot], sem.at[slot]).wait()


def coded(acc):
    top = jnp.maximum(jnp.max(jnp.abs(acc), axis=0, keepdims=True), 1e-30)
    e = jnp.ceil(jnp.log2(top))
    q = jnp.round(acc * (jnp.exp2(-e) * TOP))
    q = jnp.clip(q, -TOP, TOP)
    return q.astype(jnp.int32).astype(jnp.int16), e


def scales(rows):
    return jnp.exp2(rows.astype(jnp.int32).astype(jnp.float32)) * (1.0 / TOP)


def reduce_kernel(m, *refs, parts, side, d, first, count, arrived, last):
    refs = list(refs)
    weights = [refs.pop(0) for _ in range(parts)]
    recv = [refs.pop(0) for _ in arrived]
    if last:
        mine = refs.pop(0)
        outs = [refs.pop(0) for _ in range(count - 1)]
    else:
        out = refs.pop(0)
    if last:
        held = refs.pop(0)
    wbuf, sem, es, *sin = refs
    n = m.shape[0]

    start_weights(weights, wbuf, sem, side, 0, d, first, count)
    for r, s, (_, rows) in zip(recv, sin, arrived):
        s[...] = scales(r[rows * n :, :])

    def piece(k, added):
        wait_weight(weights, wbuf, sem, k)
        acc = jnp.dot(m[...], wbuf[k], preferred_element_type=jnp.float32)
        for r, s, (start, _) in added:
            h = k + (first - start)
            at = pl.ds(pl.multiple_of(h * n, n), n)
            acc = acc + r[at, :].astype(jnp.int32).astype(jnp.float32) * s[pl.ds(h, 1), :]
        return acc

    sums = list(zip(recv, sin, arrived))
    if last:
        mine[...] = piece(0, sums)
        size = n + EXTRA

        def code(k, _):
            q, e = coded(piece(k, sums))
            at = pl.multiple_of((k - 1) * size, EXTRA)
            held[pl.ds(at, n), :] = q
            held[pl.ds(pl.multiple_of(at + n, EXTRA), EXTRA), :] = (
                jnp.broadcast_to(e, (EXTRA, n)).astype(jnp.int32).astype(jnp.int16)
            )
            return 0

        lax.fori_loop(1, count, code, 0)
        for k, out in enumerate(outs):
            out[...] = held[k * size : (k + 1) * size, :]
        return

    es[...] = jnp.zeros_like(es)

    def body(k, _, added):
        q, e = coded(piece(k, added))
        out[pl.ds(pl.multiple_of(k * n, n), n), :] = q
        es[pl.ds(k, 1), :] = e
        return 0

    cuts = sorted({0, count, *(v for a, h in arrived for v in (a - first, a - first + h))})
    for lo, hi in zip(cuts, cuts[1:]):
        added = [t for t in sums if t[2][0] - first <= lo and hi <= t[2][0] - first + t[2][1]]
        lax.fori_loop(lo, hi, functools.partial(body, added=added), 0, unroll=1 if len(cuts) > 2 else 2)
    out[count * n :, :] = es[...].astype(jnp.int32).astype(jnp.int16)


def reduce_step(masked, weights, recv, arrived, side, d, first, count, last=False):
    tokens, width = masked.shape
    n = tokens
    if last:
        out_shape = [pltpu.VMEM((tokens, n), jnp.float32)] + [
            pltpu.VMEM((tokens + EXTRA, n), jnp.int16) for _ in range(count - 1)
        ]
    else:
        out_shape = pltpu.VMEM((count * tokens + EXTRA, n), jnp.int16)
    return pl.pallas_call(
        functools.partial(
            reduce_kernel,
            parts=len(weights),
            side=side,
            d=d,
            first=first,
            count=count,
            arrived=arrived,
            last=last,
        ),
        out_shape=out_shape,
        in_specs=[ALL_VMEM] + [HBM] * len(weights) + [ALL_VMEM] * len(recv),
        out_specs=[ALL_VMEM] * count if last else ALL_VMEM,
        scratch_shapes=([pltpu.VMEM(((count - 1) * (n + EXTRA), n), jnp.int16)] if last else [])
        + [
            pltpu.VMEM((count, width, n), masked.dtype),
            pltpu.SemaphoreType.DMA((count,)),
        ]
        + [pltpu.VMEM((EXTRA, n), jnp.float32) for _ in range(1 + len(recv))],
        compiler_params=PARAMS,
        cost_estimate=pl.CostEstimate(
            flops=2 * tokens * n * width * count,
            bytes_accessed=count * n * (width + tokens * 2) * 2,
            transcendentals=0,
        ),
    )(vmem(masked), *weights, *map(vmem, recv))


def gather_kernel(acc, *refs, parts, side, held, last):
    refs = list(refs)
    weights = [refs.pop(0) for _ in range(parts)]
    chunks = [refs.pop(0) for _ in held]
    if last:
        extra, live = refs.pop(0), refs.pop(0)
    out, total, wbuf, sem = refs
    n = acc.shape[1]
    each = held[0][2]
    for h, (d, first, count) in enumerate(held):
        start_weights(weights, wbuf, sem, side, h * each, d, first, count)
    total[...] = acc[...]

    def body(k, _):
        at = pl.ds(pl.multiple_of(k * n, n), n)
        for h, x in enumerate(chunks):
            wait_weight(weights, wbuf, sem, h * each + k)
            total[...] += lax.dot_general(
                wbuf[h * each + k],
                x[at, :],
                (((1,), (1,)), ((), ())),
                preferred_element_type=jnp.float32,
            )
        return 0

    lax.fori_loop(0, each, body, 0, unroll=2 // len(held))
    result = total[...]
    if last:
        result = live[...] * (result + adapter_scale * extra[...])
    out[...] = result.astype(out.dtype)


def gather_step(acc, weights, chunks, held, side, extra=()):
    width, tokens = acc.shape
    count = sum(c for _, _, c in held)
    last = len(extra) > 0
    return pl.pallas_call(
        functools.partial(
            gather_kernel, parts=len(weights), side=side, held=held, last=last
        ),
        out_shape=pltpu.VMEM(acc.shape, jnp.bfloat16 if last else jnp.float32),
        in_specs=[ALL_VMEM]
        + [HBM] * len(weights)
        + [ALL_VMEM] * (len(chunks) + len(extra)),
        out_specs=ALL_VMEM,
        scratch_shapes=[
            pltpu.VMEM(acc.shape, jnp.float32),
            pltpu.VMEM((count, width, tokens), jnp.bfloat16),
            pltpu.SemaphoreType.DMA((count,)),
        ],
        compiler_params=PARAMS,
        cost_estimate=pl.CostEstimate(
            flops=2 * tokens * tokens * width * count,
            bytes_accessed=count * tokens * (width + tokens) * 2,
            transcendentals=0,
        ),
    )(vmem(acc), *weights, *map(vmem, chunks), *map(vmem, extra))


def finish_kernel(mine, extra, *refs):
    *parts, out = refs
    n = mine.shape[0]
    total = mine[...] + adapter_scale * extra[...]
    for r in parts:
        s = scales(r[n:, :])[0:1, :]
        total = total + r[:n, :].astype(jnp.int32).astype(jnp.float32) * s
    out[...] = total.astype(out.dtype)


def finish(mine, extra, parts):
    return pl.pallas_call(
        finish_kernel,
        out_shape=jax.ShapeDtypeStruct(mine.shape, jnp.bfloat16),
        in_specs=[ALL_VMEM] * (2 + len(parts)),
        out_specs=ALL_VMEM,
        compiler_params=PARAMS,
    )(*map(vmem, (mine, extra, *parts)))


def low_kernel(member_blocks, tokens, masked, own, other, sums, chosen):
    each, rank, _ = own.shape
    n = tokens.shape[1]
    blocks = chosen.shape[0]
    c = lax.axis_index("dp").astype(jnp.int32)
    for b in range(blocks):
        end, member = jnp.int32(0), jnp.int32(0)
        for m in range(2 * each - 1):
            end = end + member_blocks[m]
            member = member + (end <= c * blocks + b).astype(jnp.int32)
        half = (member >= each).astype(jnp.int32)
        at = member - half * each
        factors = jnp.where(half == c, own[at], other[at])
        chosen[b] = factors
        rows = slice(b * BLOCK, (b + 1) * BLOCK)
        for k, (x, f) in enumerate(((tokens, factors[:, :n]), (masked, factors[:, n:]))):
            sums[rows, k * rank : (k + 1) * rank] = lax.dot_general(
                x[rows, :], f, (((1,), (1,)), ((), ())), preferred_element_type=jnp.float32
            )


def low_parts(member_blocks, tokens, masked, own, other):
    blocks = tokens.shape[0] // BLOCK
    return pl.pallas_call(
        low_kernel,
        out_shape=[
            pltpu.VMEM((tokens.shape[0], 2 * own.shape[1]), jnp.float32),
            pltpu.VMEM((blocks, *own.shape[1:]), own.dtype),
        ],
        in_specs=[pl.BlockSpec(memory_space=pltpu.SMEM)] + [ALL_VMEM] * 4,
        out_specs=[ALL_VMEM] * 2,
        compiler_params=PARAMS,
        cost_estimate=pl.CostEstimate(
            flops=2 * tokens.shape[0] * own[0].size, bytes_accessed=4 * own.size, transcendentals=0
        ),
    )(member_blocks, *map(vmem, (tokens, masked, own, other)))


def block_members(member_blocks, first, count):
    ends = jnp.cumsum(member_blocks)
    blocks = first + jnp.arange(count, dtype=jnp.int32)
    return jnp.sum((ends[None, :] <= blocks[:, None]).astype(jnp.int32), axis=1)


def exchange(x, side, bit, bulk):
    pairs = []
    for c in range(2):
        for y in range(side):
            for x_at in range(side):
                along_y = (c == 0) == bulk
                to_y, to_x = (y ^ bit, x_at) if along_y else (y, x_at ^ bit)
                pairs.append(
                    ((c * side + y) * side + x_at, (c * side + to_y) * side + to_x)
                )
    return lax.ppermute(x, GROUP, pairs)


def tie(*arrays):
    return lax.optimization_barrier(arrays)


def local(tokens, weight, adapter_in, adapter_out, cotangent, member_blocks, block_live, *, side):
    token_rows, width_local = tokens.shape
    hidden_local = weight.shape[1]
    blocks_here = token_rows // BLOCK
    c = lax.axis_index("dp").astype(jnp.int32)
    far = side // 2

    other = swap(weight.T)
    weights = [pltpu.with_memory_space_constraint(w, pltpu.HBM) for w in (weight.T, other)]

    factors = jnp.concatenate([adapter_in.transpose(0, 2, 1), adapter_out], axis=2)
    other_factors = swap(factors)

    def near(x, step):
        return send(x, side, step, False)

    piece = {0: tokens, 1: near(tokens, 1), side - 1: near(tokens, -1)}
    offsets = jnp.arange(BLOCK, dtype=jnp.int32)
    live = (offsets[None, :] < block_live[:, None]).astype(jnp.bfloat16).reshape(token_rows, 1)
    masked = cotangent * live

    def reduce(masked, recv, arrived, **what):
        return tie(reduce_step(masked, weights, recv, arrived, side, **what), masked)

    def gather(masked, total, chunks, held, extra=()):
        total, masked = tie(total, masked)
        return tie(gather_step(total, weights, chunks, held, side, extra), masked)

    up, masked = reduce(masked, [], (), d=far, first=0, count=far)
    down, masked = reduce(masked, [], (), d=-far, first=far, count=far)
    up, down = send(up, side, 1, True), send(down, side, -1, True)
    below = jnp.concatenate([piece[0], piece[1]], axis=0)
    above = jnp.concatenate([piece[0], piece[side - 1]], axis=0)
    below, above = near(below, 2), near(above, -2)
    piece[2], piece[3] = below[:token_rows], below[token_rows:]
    piece[side - 2], piece[side - 3] = above[:token_rows], above[token_rows:]
    piece[4] = near(piece[3], 1)
    *pieces, masked = tie(*(piece[i] for i in range(side)), masked)
    home = jnp.concatenate(pieces, axis=0)
    ahead = send(home, side, 1, True)
    behind = send(home, side, -1, True)

    sums, chosen = low_parts(member_blocks, tokens, masked, factors, other_factors)
    sums, masked = tie(sums, masked)
    rank = factors.shape[1]
    chosen_in, chosen_out = chosen[:, :, :width_local], chosen[:, :, width_local:]
    token_blocks = tokens.reshape(blocks_here, BLOCK, width_local)
    grad_blocks = masked.reshape(blocks_here, BLOCK, hidden_local)
    bits = [1 << k for k in range(side.bit_length() - 1)]

    total = jnp.zeros((hidden_local, token_rows), jnp.float32)
    total, masked = gather(masked, total, [home], ((0, 0, side),))
    held_up, held_down = (0, far), (far, far)
    moved = None
    for k in range(1, far):
        if k <= len(bits):
            if moved is not None:
                sums, masked = tie(sums + moved, masked)
            moved = exchange(sums, side, bits[k - 1], True)
        up, masked = reduce(masked, [up], (held_up,), d=far - k, first=0, count=side)
        up = send(up, side, 1, True)
        down, masked = reduce(masked, [down], (held_down,), d=k - far, first=0, count=side)
        down = send(down, side, -1, True)
        held_up = held_down = (0, side)
        ahead, behind, masked = tie(ahead, behind, masked)
        there, back = ahead, behind
        if k + 1 == far:
            ahead = ahead[: ahead.shape[0] // 2]
            behind = behind[behind.shape[0] // 2 :]
        ahead = send(ahead, side, 1, True)
        behind = send(behind, side, -1, True)
        if k <= len(bits):
            sums, masked = tie(sums + moved, masked)
            moved = exchange(sums, side, bits[k - 1], False)
        total, masked = gather(masked, total, [there, back], ((-k, 0, side), (k, 0, side)))
    sums, masked = tie((sums + moved).astype(jnp.bfloat16), masked)
    low_in = sums[:, :rank].reshape(blocks_here, BLOCK, rank)
    low_back = sums[:, rank:].reshape(blocks_here, BLOCK, rank)
    mine, *leaving = reduce_step(
        masked,
        weights,
        [up, down],
        (held_up, held_down),
        side,
        d=0,
        first=0,
        count=side,
        last=True,
    )
    *leaving, mine, masked = tie(*leaving, mine, masked)
    arrived = [
        send(a, side, -s if s <= far else side - s, False)
        for s, a in enumerate(leaving, start=1)
    ]

    raised = jnp.einsum("btr,brf->fbt", low_in, chosen_out, preferred_element_type=jnp.float32)
    hidden, masked = gather(
        masked,
        total,
        [ahead, behind],
        ((-far, 0, far), (far, far, far)),
        extra=(
            raised.reshape(hidden_local, token_rows),
            live.astype(jnp.float32).reshape(1, token_rows),
        ),
    )
    hidden = hidden.T
    reduced = jnp.einsum("btr,brk->btk", low_back, chosen_in, preferred_element_type=jnp.float32)
    input_gradient = finish(mine, reduced.reshape(token_rows, width_local), arrived)

    down_outer = jnp.einsum(
        "btr,btk->brk", low_back, token_blocks, preferred_element_type=jnp.float32
    )
    up_outer = jnp.einsum("btr,btf->brf", low_in, grad_blocks, preferred_element_type=jnp.float32)
    outer = jnp.concatenate([down_outer, up_outer], axis=2)
    members = block_members(member_blocks, c * blocks_here, blocks_here)
    held_here = MEMBERS // 2

    def of_members(first):
        owners = first + jnp.arange(held_here, dtype=jnp.int32)
        picked = (owners[:, None] == members[None, :])[:, :, None, None]
        return adapter_scale * jnp.where(picked, outer[None], 0.0).sum(axis=1)

    grads = of_members(c * held_here) + swap(of_members((1 - c) * held_here))
    down_grad = grads[:, :, :width_local].transpose(0, 2, 1)
    return (hidden, input_gradient, down_grad, grads[:, :, width_local:])


def solution(mesh):
    side = math.isqrt(mesh.shape["tensor"])
    assert side == 8 and side * side == mesh.shape["tensor"] and mesh.shape["dp"] == 2
    finer = Mesh(
        mesh.devices.reshape(mesh.shape["pop"], mesh.shape["dp"], side, side),
        ("pop", "dp", "ty", "tx"),
    )
    placed = (
        P(("pop", "dp"), TENSOR),
        P("dp", TENSOR),
        P(("pop", "dp"), TENSOR, None),
        P(("pop", "dp"), None, TENSOR),
        P(("pop", "dp"), TENSOR),
        P("pop"),
        P(("pop", "dp")),
    )

    def body(*args):
        return local(*args, side=side)

    return jax.shard_map(
        body,
        mesh=finer,
        in_specs=placed,
        out_specs=(
            P(("pop", "dp"), TENSOR),
            P(("pop", "dp"), TENSOR),
            P(("pop", "dp"), TENSOR, None),
            P(("pop", "dp"), None, TENSOR),
        ),
        check_vma=False,
    )
```

profile of v0, /device:TPU:518, one launch (start us, length us, event | category | flops | bytes accessed | tf_op | source)
XLA Modules:
  0.0 229.3 jit_solution(56713728234465106)
XLA Ops:
  0.8 3.0 %collective-permute-start = (bf16[256,256]{1,0:T(8,128)(2,1)}, bf16[256,256]{1,0:T(8,128)(2,1)S(1)}, u32[]{:S(2)}, u32[]{:S(2)}) collective-permute-start(bf16[256,256]{1,0:T(8,128)(2,1)} %tokens.1), channel_id=1, source_target_pairs={{0,1},{1,2},{2,3},{3,4},{4,5},{5,6},{6,7},{7,0},{8,9},{9,10},{10,1... | collective-permute-start | bytes 393224 | tf_op jit(solution)/shard_map/ppermute | solution.py:38
  6.6 3.5 %collective-permute-done.3 = bf16[256,256]{1,0:T(8,128)(2,1)S(1)} collective-permute-done((bf16[256,256]{1,0:T(8,128)(2,1)}, bf16[256,256]{1,0:T(8,128)(2,1)S(1)}, u32[]{:S(2)}, u32[]{:S(2)}) %collective-permute-start.3) | collective-permute-done | bytes 131104 | tf_op jit(solution)/shard_map/ppermute | solution.py:38
  12.1 13.7 %collective-permute-start.4 = (bf16[512,256]{1,0:T(8,128)(2,1)S(1)}, bf16[512,256]{1,0:T(8,128)(2,1)S(1)}, u32[]{:S(2)}, u32[]{:S(2)}) collective-permute-start(bf16[512,256]{1,0:T(8,128)(2,1)S(1)} %get-tuple-element.174), channel_id=1, source_target_pairs={{0,6},{1,7},{2,0},{3,1},{4,2},{5,3},{6,4},{7,5},{8,14},{9,15},{10,... | collective-permute-start | bytes 786440 | tf_op jit(solution)/shard_map/ppermute | solution.py:38
  25.9 6.0 %collective-permute-done.1 = bf16[512,256]{1,0:T(8,128)(2,1)S(1)} collective-permute-done((bf16[512,256]{1,0:T(8,128)(2,1)S(1)}, bf16[512,256]{1,0:T(8,128)(2,1)S(1)}, u32[]{:S(2)}, u32[]{:S(2)}) %collective-permute-start.1) | collective-permute-done | bytes 262176 | tf_op jit(solution)/shard_map/ppermute | solution.py:38
  32.0 7.1 %collective-permute-done.4 = bf16[512,256]{1,0:T(8,128)(2,1)S(1)} collective-permute-done((bf16[512,256]{1,0:T(8,128)(2,1)S(1)}, bf16[512,256]{1,0:T(8,128)(2,1)S(1)}, u32[]{:S(2)}, u32[]{:S(2)}) %collective-permute-start.4) | collective-permute-done | bytes 262176 | tf_op jit(solution)/shard_map/ppermute | solution.py:38
  44.3 3.2 %collective-permute-start.9 = (bf16[2048,256]{1,0:T(8,128)(2,1)S(1)}, bf16[2048,256]{1,0:T(8,128)(2,1)S(1)}, u32[]{:S(2)}, u32[]{:S(2)}) collective-permute-start(bf16[2048,256]{1,0:T(8,128)(2,1)S(1)} %constant_dynamic-update-slice_fusion.refs_2_), channel_id=1, source_target_pairs={{0,56},{1,57},{2,58},{3,59},{4,60},{5,61},{6,62},{7,63},{8,0},{9,1... | collective-permute-start | bytes 3145736 | tf_op jit(solution)/shard_map/ppermute | solution.py:38
  47.5 3.2 %collective-permute-start.11 = (s16[1040,256]{1,0:T(8,128)(2,1)S(1)}, s16[1040,256]{1,0:T(8,128)(2,1)S(1)}, u32[]{:S(2)}, u32[]{:S(2)}) collective-permute-start(s16[1040,256]{1,0:T(8,128)(2,1)S(1)} %shard_map.103), channel_id=1, source_target_pairs={{0,56},{1,57},{2,58},{3,59},{4,60},{5,61},{6,62},{7,63},{8,0},{9,1... | collective-permute-start | bytes 1597448 | tf_op jit(solution)/shard_map/ppermute | solution.py:38
  53.3 3.4 %shard_map.105.acc = f32[416,256]{1,0:T(8,128)S(1)} custom-call(f32[416,256]{1,0:T(8,128)S(1)} %broadcast_in_dim.44.acc, bf16[416,8192]{1,0:T(8,128)(2,1)} %bitcast.37, bf16[416,8192]{1,0:T(8,128)(2,1)} %collective-permute-done.5.refs_1_, bf16[2048,256]{1,0:T(8,128)(2,1)S(1)} %constant_dynamic-update-slice_fusion.refs_2_), custom_call_target="tpu_custom_call" | custom-call | flops 436207616 | bytes 2752512 | tf_op jit(solution)/shard_map/pallas_call | solution.py:238
  56.7 9.3 %collective-permute-done.10.refs_2_ = s16[1040,256]{1,0:T(8,128)(2,1)S(1)} collective-permute-done((s16[1040,256]{1,0:T(8,128)(2,1)S(1)}, s16[1040,256]{1,0:T(8,128)(2,1)S(1)}, u32[]{:S(2)}, u32[]{:S(2)}) %collective-permute-start.10) | collective-permute-done | bytes 532512 | tf_op jit(solution)/shard_map/ppermute | solution.py:38
  66.0 3.3 %shard_map.106 = s16[2064,256]{1,0:T(8,128)(2,1)S(1)} custom-call(bf16[256,416]{1,0:T(8,128)(2,1)S(1)} %broadcast_multiply_fusion.1.m.masked, bf16[416,8192]{1,0:T(8,128)(2,1)} %bitcast.38, bf16[416,8192]{1,0:T(8,128)(2,1)} %collective-permute-done.5.refs_1_, s16[1040,256]{1,0:T(8,128)(2,1)S(1)} %collective-permute-done.10.refs_2_), custom_call_target="tpu_custom_call" | custom-call | flops 436207616 | bytes 3801088 | tf_op jit(solution)/shard_map/pallas_call | solution.py:173
  69.4 3.3 %shard_map.107 = s16[2064,256]{1,0:T(8,128)(2,1)S(1)} custom-call(bf16[256,416]{1,0:T(8,128)(2,1)S(1)} %broadcast_multiply_fusion.1.m.masked, bf16[416,8192]{1,0:T(8,128)(2,1)} %bitcast.39, bf16[416,8192]{1,0:T(8,128)(2,1)} %collective-permute-done.5.refs_1_, s16[1040,256]{1,0:T(8,128)(2,1)S(1)} %collective-permute-done.11.refs_2_), custom_call_target="tpu_custom_call" | custom-call | flops 436207616 | bytes 3801088 | tf_op jit(solution)/shard_map/pallas_call | solution.py:173
  72.7 3.5 %collective-permute-start.17 = (s16[2064,256]{1,0:T(8,128)(2,1)S(1)}, s16[2064,256]{1,0:T(8,128)(2,1)S(1)}, u32[]{:S(2)}, u32[]{:S(2)}) collective-permute-start(s16[2064,256]{1,0:T(8,128)(2,1)S(1)} %shard_map.107), channel_id=1, source_target_pairs={{0,56},{1,57},{2,58},{3,59},{4,60},{5,61},{6,62},{7,63},{8,0},{9,1... | collective-permute-start | bytes 3170312 | tf_op jit(solution)/shard_map/ppermute | solution.py:38
  76.2 3.2 %collective-permute-start.15 = (bf16[2048,256]{1,0:T(8,128)(2,1)S(1)}, bf16[2048,256]{1,0:T(8,128)(2,1)}, u32[]{:S(2)}, u32[]{:S(2)}) collective-permute-start(bf16[2048,256]{1,0:T(8,128)(2,1)S(1)} %collective-permute-done.9.refs_3_), channel_id=1, source_target_pairs={{0,56},{1,57},{2,58},{3,59},{4,60},{5,61},{6,62},{7,63},{8,0},{9,1... | collective-permute-start | bytes 3145736 | tf_op jit(solution)/shard_map/ppermute | solution.py:38
  79.4 22.5 %collective-permute-done.7 = f32[256,128]{1,0:T(8,128)S(1)} collective-permute-done((f32[256,128]{1,0:T(8,128)S(1)}, f32[256,128]{1,0:T(8,128)S(1)}, u32[]{:S(2)}, u32[]{:S(2)}) %collective-permute-start.7) | collective-permute-done | bytes 131104 | tf_op jit(solution)/shard_map/ppermute | solution.py:335
  102.1 6.2 %shard_map.108.acc = f32[416,256]{1,0:T(8,128)S(1)} custom-call(f32[416,256]{1,0:T(8,128)S(1)} %shard_map.105.acc, bf16[416,8192]{1,0:T(8,128)(2,1)} %bitcast.40, bf16[416,8192]{1,0:T(8,128)(2,1)} %collective-permute-done.5.refs_1_, bf16[2048,256]{1,0:T(8,128)(2,1)S(1)} %collective-permute-done.8.refs_2_, bf16[2048,256]{1,0:T(8,128)(2,1)S(1)} %collective-permute-done.9.refs_3_), custom_call_target="tpu_custom_call" | custom-call | flops 872415232 | bytes 5505024 | tf_op jit(solution)/shard_map/pallas_call | solution.py:238
  108.4 4.8 %shard_map.109 = s16[2064,256]{1,0:T(8,128)(2,1)} custom-call(bf16[256,416]{1,0:T(8,128)(2,1)S(1)} %broadcast_multiply_fusion.1.m.masked, bf16[416,8192]{1,0:T(8,128)(2,1)} %bitcast.41, bf16[416,8192]{1,0:T(8,128)(2,1)} %collective-permute-done.5.refs_1_, s16[2064,256]{1,0:T(8,128)(2,1)S(1)} %collective-permute-done.16.refs_2_), custom_call_target="tpu_custom_call" | custom-call | flops 436207616 | bytes 3801088 | tf_op jit(solution)/shard_map/pallas_call | solution.py:173
  113.4 4.7 %shard_map.110 = s16[2064,256]{1,0:T(8,128)(2,1)} custom-call(bf16[256,416]{1,0:T(8,128)(2,1)S(1)} %broadcast_multiply_fusion.1.m.masked, bf16[416,8192]{1,0:T(8,128)(2,1)} %bitcast.42, bf16[416,8192]{1,0:T(8,128)(2,1)} %collective-permute-done.5.refs_1_, s16[2064,256]{1,0:T(8,128)(2,1)S(1)} %collective-permute-done.17.refs_2_), custom_call_target="tpu_custom_call" | custom-call | flops 436207616 | bytes 3801088 | tf_op jit(solution)/shard_map/pallas_call | solution.py:173
  118.1 3.3 %collective-permute-start.23 = (s16[2064,256]{1,0:T(8,128)(2,1)}, s16[2064,256]{1,0:T(8,128)(2,1)}, u32[]{:S(2)}, u32[]{:S(2)}) collective-permute-start(s16[2064,256]{1,0:T(8,128)(2,1)} %shard_map.110), channel_id=1, source_target_pairs={{0,56},{1,57},{2,58},{3,59},{4,60},{5,61},{6,62},{7,63},{8,0},{9,1... | collective-permute-start | bytes 3170312 | tf_op jit(solution)/shard_map/ppermute | solution.py:38
  121.4 3.2 %collective-permute-start.21 = (bf16[2048,256]{1,0:T(8,128)(2,1)}, bf16[2048,256]{1,0:T(8,128)(2,1)S(1)}, u32[]{:S(2)}, u32[]{:S(2)}) collective-permute-start(bf16[2048,256]{1,0:T(8,128)(2,1)} %collective-permute-done.15.refs_3_), channel_id=1, source_target_pairs={{0,56},{1,57},{2,58},{3,59},{4,60},{5,61},{6,62},{7,63},{8,0},{9,1... | collective-permute-start | bytes 3145736 | tf_op jit(solution)/shard_map/ppermute | solution.py:38
  124.6 24.4 %collective-permute-done.13 = f32[256,128]{1,0:T(8,128)S(1)} collective-permute-done((f32[256,128]{1,0:T(8,128)S(1)}, f32[256,128]{1,0:T(8,128)S(1)}, u32[]{:S(2)}, u32[]{:S(2)}) %collective-permute-start.13) | collective-permute-done | bytes 131104 | tf_op jit(solution)/shard_map/ppermute | solution.py:335
  151.5 7.7 %shard_map.111.acc = f32[416,256]{1,0:T(8,128)S(1)} custom-call(f32[416,256]{1,0:T(8,128)S(1)} %shard_map.108.acc, bf16[416,8192]{1,0:T(8,128)(2,1)} %bitcast.43, bf16[416,8192]{1,0:T(8,128)(2,1)} %collective-permute-done.5.refs_1_, bf16[2048,256]{1,0:T(8,128)(2,1)} %collective-permute-done.14.refs_2_, bf16[2048,256]{1,0:T(8,128)(2,1)} %collective-permute-done.15.refs_3_), custom_call_target="tpu_custom_call" | custom-call | flops 872415232 | bytes 5505024 | tf_op jit(solution)/shard_map/pallas_call | solution.py:238
  160.2 7.1 %collective-permute-start.19 = (f32[256,128]{1,0:T(8,128)S(1)}, f32[256,128]{1,0:T(8,128)S(1)}, u32[]{:S(2)}, u32[]{:S(2)}) collective-permute-start(f32[256,128]{1,0:T(8,128)S(1)} %add.46), channel_id=1, source_target_pairs={{0,32},{1,33},{2,34},{3,35},{4,36},{5,37},{6,38},{7,39},{8,40},{9,... | collective-permute-start | bytes 393224 | tf_op jit(solution)/shard_map/ppermute | solution.py:335
  167.6 4.4 %collective-permute-done.19 = f32[256,128]{1,0:T(8,128)S(1)} collective-permute-done((f32[256,128]{1,0:T(8,128)S(1)}, f32[256,128]{1,0:T(8,128)S(1)}, u32[]{:S(2)}, u32[]{:S(2)}) %collective-permute-start.19) | collective-permute-done | bytes 131104 | tf_op jit(solution)/shard_map/ppermute | solution.py:335
  172.1 5.0 %shard_map.112 = s16[2064,256]{1,0:T(8,128)(2,1)S(1)} custom-call(bf16[256,416]{1,0:T(8,128)(2,1)S(1)} %broadcast_multiply_fusion.1.m.masked, bf16[416,8192]{1,0:T(8,128)(2,1)} %bitcast.44, bf16[416,8192]{1,0:T(8,128)(2,1)} %collective-permute-done.5.refs_1_, s16[2064,256]{1,0:T(8,128)(2,1)} %collective-permute-done.22.refs_2_), custom_call_target="tpu_custom_call" | custom-call | flops 436207616 | bytes 3801088 | tf_op jit(solution)/shard_map/pallas_call | solution.py:173
  177.1 5.0 %shard_map.113 = s16[2064,256]{1,0:T(8,128)(2,1)S(1)} custom-call(bf16[256,416]{1,0:T(8,128)(2,1)S(1)} %broadcast_multiply_fusion.1.m.masked, bf16[416,8192]{1,0:T(8,128)(2,1)} %bitcast.45, bf16[416,8192]{1,0:T(8,128)(2,1)} %collective-permute-done.5.refs_1_, s16[2064,256]{1,0:T(8,128)(2,1)} %collective-permute-done.23.refs_2_), custom_call_target="tpu_custom_call" | custom-call | flops 436207616 | bytes 3801088 | tf_op jit(solution)/shard_map/pallas_call | solution.py:173
  184.8 3.2 %collective-permute-start.28 = (s16[2064,256]{1,0:T(8,128)(2,1)S(1)}, s16[2064,256]{1,0:T(8,128)(2,1)S(1)}, u32[]{:S(2)}, u32[]{:S(2)}) collective-permute-start(s16[2064,256]{1,0:T(8,128)(2,1)S(1)} %shard_map.113), channel_id=1, source_target_pairs={{0,56},{1,57},{2,58},{3,59},{4,60},{5,61},{6,62},{7,63},{8,0},{9,1... | collective-permute-start | bytes 3170312 | tf_op jit(solution)/shard_map/ppermute | solution.py:38
  188.0 6.2 %shard_map.114.acc = f32[416,256]{1,0:T(8,128)S(1)} custom-call(f32[416,256]{1,0:T(8,128)S(1)} %shard_map.111.acc, bf16[416,8192]{1,0:T(8,128)(2,1)} %bitcast.46, bf16[416,8192]{1,0:T(8,128)(2,1)} %collective-permute-done.5.refs_1_, bf16[2048,256]{1,0:T(8,128)(2,1)S(1)} %collective-permute-done.20.refs_2_, bf16[2048,256]{1,0:T(8,128)(2,1)S(1)} %collective-permute-done.21.refs_3_), custom_call_target="tpu_custom_call" | custom-call | flops 872415232 | bytes 5505024 | tf_op jit(solution)/shard_map/pallas_call | solution.py:238
  194.4 3.2 %collective-permute-start.25 = (bf16[1024,256]{1,0:T(8,128)(2,1)S(1)}, bf16[1024,256]{1,0:T(8,128)(2,1)S(1)}, u32[]{:S(2)}, u32[]{:S(2)}) collective-permute-start(bf16[1024,256]{1,0:T(8,128)(2,1)S(1)} %slice.41), channel_id=1, source_target_pairs={{0,56},{1,57},{2,58},{3,59},{4,60},{5,61},{6,62},{7,63},{8,0},{9,1... | collective-permute-start | bytes 1572872 | tf_op jit(solution)/shard_map/ppermute | solution.py:38
  200.8 3.3 %shard_map.116 = (f32[256,256]{1,0:T(8,128)S(1)}, s16[272,256]{1,0:T(8,128)(2,1)S(1)}, s16[272,256]{1,0:T(8,128)(2,1)S(1)}, s16[272,256]{1,0:T(8,128)(2,1)S(1)},...) custom-call(bf16[256,416]{1,0:T(8,128)(2,1)S(1)} %broadcast_multiply, ...), custom_call_target="tpu_custom_call" | custom-call | flops 436207616 | bytes 3801088 | tf_op jit(solution)/shard_map/pallas_call | solution.py:173
  205.2 3.6 %collective-permute-start.31 = (s16[272,256]{1,0:T(8,128)(2,1)S(1)}, s16[272,256]{1,0:T(8,128)(2,1)S(1)}, u32[]{:S(2)}, u32[]{:S(2)}) collective-permute-start(s16[272,256]{1,0:T(8,128)(2,1)S(1)} %get-tuple-element.163), channel_id=1, source_target_pairs={{0,5},{1,6},{2,7},{3,0},{4,1},{5,2},{6,3},{7,4},{8,13},{9,14},{10,... | collective-permute-start | bytes 417800 | tf_op jit(solution)/shard_map/ppermute | solution.py:38
  213.9 3.6 %collective-permute-start.34 = (s16[272,256]{1,0:T(8,128)(2,1)S(1)}, s16[272,256]{1,0:T(8,128)(2,1)S(1)}, u32[]{:S(2)}, u32[]{:S(2)}) collective-permute-start(s16[272,256]{1,0:T(8,128)(2,1)S(1)} %get-tuple-element.166), channel_id=1, source_target_pairs={{0,2},{1,3},{2,4},{3,5},{4,6},{5,7},{6,0},{7,1},{8,10},{9,11},{10,... | collective-permute-start | bytes 417800 | tf_op jit(solution)/shard_map/ppermute | solution.py:38
  220.8 3.5 %shard_map.115 = bf16[416,256]{1,0:T(8,128)(2,1)S(1)} custom-call(f32[416,256]{1,0:T(8,128)S(1)} %shard_map.114.acc, bf16[416,8192]{1,0:T(8,128)(2,1)} %bitcast.48, bf16[416,8192]{1,0:T(8,128)(2,1)} %collective-permute-done.5.refs_1_, bf16[1024,256]{1,0:T(8,128)(2,1)S(1)} %collective-permute-done.24.refs_2_, ...), custom_call_target="tpu_custom_call" | custom-call | flops 436207616 | bytes 2752512 | tf_op jit(solution)/shard_map/pallas_call | solution.py:238
  (109 shorter events, 37.7 us)
Async XLA Ops:
  0.6 38.5 %collective-permute-start.5 = (bf16[416,8192]{1,0:T(8,128)(2,1)}, bf16[416,8192]{1,0:T(8,128)(2,1)}, u32[]{:S(2)}, u32[]{:S(2)}) collective-permute-start(bf16[416,8192]{1,0:T(8,128)(2,1)} %bitcast.34), channel_id=1, source_target_pairs={{0,64},{64,0},{1,65},{65,1},{2,66},{66,2},{3,67},{67,3},{4,68},{68... | collective-permute-start | bytes 20447240 | tf_op jit(solution)/shard_map/ppermute | solution.py:42
  11.1 20.8 %collective-permute-start.1 = (bf16[512,256]{1,0:T(8,128)(2,1)S(1)}, bf16[512,256]{1,0:T(8,128)(2,1)S(1)}, u32[]{:S(2)}, u32[]{:S(2)}) collective-permute-start(bf16[512,256]{1,0:T(8,128)(2,1)S(1)} %get-tuple-element.175), channel_id=1, source_target_pairs={{0,2},{1,3},{2,4},{3,5},{4,6},{5,7},{6,0},{7,1},{8,10},{9,11},{10,... | collective-permute-start | bytes 786440 | tf_op jit(solution)/shard_map/ppermute | solution.py:38
  12.1 27.0 %collective-permute-start.4 = (bf16[512,256]{1,0:T(8,128)(2,1)S(1)}, bf16[512,256]{1,0:T(8,128)(2,1)S(1)}, u32[]{:S(2)}, u32[]{:S(2)}) collective-permute-start(bf16[512,256]{1,0:T(8,128)(2,1)S(1)} %get-tuple-element.174), channel_id=1, source_target_pairs={{0,6},{1,7},{2,0},{3,1},{4,2},{5,3},{6,4},{7,5},{8,14},{9,15},{10,... | collective-permute-start | bytes 786440 | tf_op jit(solution)/shard_map/ppermute | solution.py:38
  31.9 12.1 %collective-permute-start.2 = (bf16[256,256]{1,0:T(8,128)(2,1)S(1)}, bf16[256,256]{1,0:T(8,128)(2,1)S(1)}, u32[]{:S(2)}, u32[]{:S(2)}) collective-permute-start(bf16[256,256]{1,0:T(8,128)(2,1)S(1)} %get-tuple-element.95), channel_id=1, source_target_pairs={{0,1},{1,2},{2,3},{3,4},{4,5},{5,6},{6,7},{7,0},{8,9},{9,10},{10,1... | collective-permute-start | bytes 393224 | tf_op jit(solution)/shard_map/ppermute | solution.py:38
  44.1 32.0 %collective-permute-start.8 = (bf16[2048,256]{1,0:T(8,128)(2,1)S(1)}, bf16[2048,256]{1,0:T(8,128)(2,1)S(1)}, u32[]{:S(2)}, u32[]{:S(2)}) collective-permute-start(bf16[2048,256]{1,0:T(8,128)(2,1)S(1)} %constant_dynamic-update-slice_fusion.refs_2_), channel_id=1, source_target_pairs={{0,8},{1,9},{2,10},{3,11},{4,12},{5,13},{6,14},{7,15},{8,16},{9,17... | collective-permute-start | bytes 3145736 | tf_op jit(solution)/shard_map/ppermute | solution.py:38
  44.3 31.9 %collective-permute-start.9 = (bf16[2048,256]{1,0:T(8,128)(2,1)S(1)}, bf16[2048,256]{1,0:T(8,128)(2,1)S(1)}, u32[]{:S(2)}, u32[]{:S(2)}) collective-permute-start(bf16[2048,256]{1,0:T(8,128)(2,1)S(1)} %constant_dynamic-update-slice_fusion.refs_2_), channel_id=1, source_target_pairs={{0,56},{1,57},{2,58},{3,59},{4,60},{5,61},{6,62},{7,63},{8,0},{9,1... | collective-permute-start | bytes 3145736 | tf_op jit(solution)/shard_map/ppermute | solution.py:38
  47.5 18.5 %collective-permute-start.10 = (s16[1040,256]{1,0:T(8,128)(2,1)S(1)}, s16[1040,256]{1,0:T(8,128)(2,1)S(1)}, u32[]{:S(2)}, u32[]{:S(2)}) collective-permute-start(s16[1040,256]{1,0:T(8,128)(2,1)S(1)} %shard_map.102), channel_id=1, source_target_pairs={{0,8},{1,9},{2,10},{3,11},{4,12},{5,13},{6,14},{7,15},{8,16},{9,17... | collective-permute-start | bytes 1597448 | tf_op jit(solution)/shard_map/ppermute | solution.py:38
  47.5 21.9 %collective-permute-start.11 = (s16[1040,256]{1,0:T(8,128)(2,1)S(1)}, s16[1040,256]{1,0:T(8,128)(2,1)S(1)}, u32[]{:S(2)}, u32[]{:S(2)}) collective-permute-start(s16[1040,256]{1,0:T(8,128)(2,1)S(1)} %shard_map.103), channel_id=1, source_target_pairs={{0,56},{1,57},{2,58},{3,59},{4,60},{5,61},{6,62},{7,63},{8,0},{9,1... | collective-permute-start | bytes 1597448 | tf_op jit(solution)/shard_map/ppermute | solution.py:38
  69.2 39.2 %collective-permute-start.16 = (s16[2064,256]{1,0:T(8,128)(2,1)S(1)}, s16[2064,256]{1,0:T(8,128)(2,1)S(1)}, u32[]{:S(2)}, u32[]{:S(2)}) collective-permute-start(s16[2064,256]{1,0:T(8,128)(2,1)S(1)} %shard_map.106), channel_id=1, source_target_pairs={{0,8},{1,9},{2,10},{3,11},{4,12},{5,13},{6,14},{7,15},{8,16},{9,17... | collective-permute-start | bytes 3170312 | tf_op jit(solution)/shard_map/ppermute | solution.py:38
  72.7 40.7 %collective-permute-start.17 = (s16[2064,256]{1,0:T(8,128)(2,1)S(1)}, s16[2064,256]{1,0:T(8,128)(2,1)S(1)}, u32[]{:S(2)}, u32[]{:S(2)}) collective-permute-start(s16[2064,256]{1,0:T(8,128)(2,1)S(1)} %shard_map.107), channel_id=1, source_target_pairs={{0,56},{1,57},{2,58},{3,59},{4,60},{5,61},{6,62},{7,63},{8,0},{9,1... | collective-permute-start | bytes 3170312 | tf_op jit(solution)/shard_map/ppermute | solution.py:38
  76.1 45.3 %collective-permute-start.14 = (bf16[2048,256]{1,0:T(8,128)(2,1)S(1)}, bf16[2048,256]{1,0:T(8,128)(2,1)}, u32[]{:S(2)}, u32[]{:S(2)}) collective-permute-start(bf16[2048,256]{1,0:T(8,128)(2,1)S(1)} %collective-permute-done.8.refs_2_), channel_id=1, source_target_pairs={{0,8},{1,9},{2,10},{3,11},{4,12},{5,13},{6,14},{7,15},{8,16},{9,17... | collective-permute-start | bytes 3145736 | tf_op jit(solution)/shard_map/ppermute | solution.py:38
  76.2 45.2 %collective-permute-start.15 = (bf16[2048,256]{1,0:T(8,128)(2,1)S(1)}, bf16[2048,256]{1,0:T(8,128)(2,1)}, u32[]{:S(2)}, u32[]{:S(2)}) collective-permute-start(bf16[2048,256]{1,0:T(8,128)(2,1)S(1)} %collective-permute-done.9.refs_3_), channel_id=1, source_target_pairs={{0,56},{1,57},{2,58},{3,59},{4,60},{5,61},{6,62},{7,63},{8,0},{9,1... | collective-permute-start | bytes 3145736 | tf_op jit(solution)/shard_map/ppermute | solution.py:38
  79.4 22.5 %collective-permute-start.7 = (f32[256,128]{1,0:T(8,128)S(1)}, f32[256,128]{1,0:T(8,128)S(1)}, u32[]{:S(2)}, u32[]{:S(2)}) collective-permute-start(f32[256,128]{1,0:T(8,128)S(1)} %get-tuple-element.102), channel_id=1, source_target_pairs={{0,8},{1,9},{2,10},{3,11},{4,12},{5,13},{6,14},{7,15},{8,0},{9,1},... | collective-permute-start | bytes 393224 | tf_op jit(solution)/shard_map/ppermute | solution.py:335
  113.2 58.8 %collective-permute-start.22 = (s16[2064,256]{1,0:T(8,128)(2,1)}, s16[2064,256]{1,0:T(8,128)(2,1)}, u32[]{:S(2)}, u32[]{:S(2)}) collective-permute-start(s16[2064,256]{1,0:T(8,128)(2,1)} %shard_map.109), channel_id=1, source_target_pairs={{0,8},{1,9},{2,10},{3,11},{4,12},{5,13},{6,14},{7,15},{8,16},{9,17... | collective-permute-start | bytes 3170312 | tf_op jit(solution)/shard_map/ppermute | solution.py:38
  118.1 58.9 %collective-permute-start.23 = (s16[2064,256]{1,0:T(8,128)(2,1)}, s16[2064,256]{1,0:T(8,128)(2,1)}, u32[]{:S(2)}, u32[]{:S(2)}) collective-permute-start(s16[2064,256]{1,0:T(8,128)(2,1)} %shard_map.110), channel_id=1, source_target_pairs={{0,56},{1,57},{2,58},{3,59},{4,60},{5,61},{6,62},{7,63},{8,0},{9,1... | collective-permute-start | bytes 3170312 | tf_op jit(solution)/shard_map/ppermute | solution.py:38
  121.4 60.6 %collective-permute-start.20 = (bf16[2048,256]{1,0:T(8,128)(2,1)}, bf16[2048,256]{1,0:T(8,128)(2,1)S(1)}, u32[]{:S(2)}, u32[]{:S(2)}) collective-permute-start(bf16[2048,256]{1,0:T(8,128)(2,1)} %collective-permute-done.14.refs_2_), channel_id=1, source_target_pairs={{0,8},{1,9},{2,10},{3,11},{4,12},{5,13},{6,14},{7,15},{8,16},{9,17... | collective-permute-start | bytes 3145736 | tf_op jit(solution)/shard_map/ppermute | solution.py:38
  121.4 60.6 %collective-permute-start.21 = (bf16[2048,256]{1,0:T(8,128)(2,1)}, bf16[2048,256]{1,0:T(8,128)(2,1)S(1)}, u32[]{:S(2)}, u32[]{:S(2)}) collective-permute-start(bf16[2048,256]{1,0:T(8,128)(2,1)} %collective-permute-done.15.refs_3_), channel_id=1, source_target_pairs={{0,56},{1,57},{2,58},{3,59},{4,60},{5,61},{6,62},{7,63},{8,0},{9,1... | collective-permute-start | bytes 3145736 | tf_op jit(solution)/shard_map/ppermute | solution.py:38
  124.6 24.4 %collective-permute-start.13 = (f32[256,128]{1,0:T(8,128)S(1)}, f32[256,128]{1,0:T(8,128)S(1)}, u32[]{:S(2)}, u32[]{:S(2)}) collective-permute-start(f32[256,128]{1,0:T(8,128)S(1)} %add.44), channel_id=1, source_target_pairs={{0,16},{1,17},{2,18},{3,19},{4,20},{5,21},{6,22},{7,23},{8,24},{9,... | collective-permute-start | bytes 393224 | tf_op jit(solution)/shard_map/ppermute | solution.py:335
  149.7 9.5 %collective-permute-start.18 = (f32[256,128]{1,0:T(8,128)}, f32[256,128]{1,0:T(8,128)}, u32[]{:S(2)}, u32[]{:S(2)}) collective-permute-start(f32[256,128]{1,0:T(8,128)} %add.45), channel_id=1, source_target_pairs={{0,2},{1,3},{2,0},{3,1},{4,6},{5,7},{6,4},{7,5},{8,10},{9,11},{10,... | collective-permute-start | bytes 393224 | tf_op jit(solution)/shard_map/ppermute | solution.py:335
  160.2 11.8 %collective-permute-start.19 = (f32[256,128]{1,0:T(8,128)S(1)}, f32[256,128]{1,0:T(8,128)S(1)}, u32[]{:S(2)}, u32[]{:S(2)}) collective-permute-start(f32[256,128]{1,0:T(8,128)S(1)} %add.46), channel_id=1, source_target_pairs={{0,32},{1,33},{2,34},{3,35},{4,36},{5,37},{6,38},{7,39},{8,40},{9,... | collective-permute-start | bytes 393224 | tf_op jit(solution)/shard_map/ppermute | solution.py:335
  182.1 15.5 %collective-permute-start.26 = (f32[256,128]{1,0:T(8,128)S(1)}, f32[256,128]{1,0:T(8,128)S(1)}, u32[]{:S(2)}, u32[]{:S(2)}) collective-permute-start(f32[256,128]{1,0:T(8,128)S(1)} %add.47), channel_id=1, source_target_pairs={{0,4},{1,5},{2,6},{3,7},{4,0},{5,1},{6,2},{7,3},{8,12},{9,13},{10,... | collective-permute-start | bytes 393224 | tf_op jit(solution)/shard_map/ppermute | solution.py:335
  184.5 16.4 %collective-permute-start.27 = (s16[2064,256]{1,0:T(8,128)(2,1)S(1)}, s16[2064,256]{1,0:T(8,128)(2,1)S(1)}, u32[]{:S(2)}, u32[]{:S(2)}) collective-permute-start(s16[2064,256]{1,0:T(8,128)(2,1)S(1)} %shard_map.112), channel_id=1, source_target_pairs={{0,8},{1,9},{2,10},{3,11},{4,12},{5,13},{6,14},{7,15},{8,16},{9,17... | collective-permute-start | bytes 3170312 | tf_op jit(solution)/shard_map/ppermute | solution.py:38
  184.8 16.1 %collective-permute-start.28 = (s16[2064,256]{1,0:T(8,128)(2,1)S(1)}, s16[2064,256]{1,0:T(8,128)(2,1)S(1)}, u32[]{:S(2)}, u32[]{:S(2)}) collective-permute-start(s16[2064,256]{1,0:T(8,128)(2,1)S(1)} %shard_map.113), channel_id=1, source_target_pairs={{0,56},{1,57},{2,58},{3,59},{4,60},{5,61},{6,62},{7,63},{8,0},{9,1... | collective-permute-start | bytes 3170312 | tf_op jit(solution)/shard_map/ppermute | solution.py:38
  194.2 14.5 %collective-permute-start.24 = (bf16[1024,256]{1,0:T(8,128)(2,1)S(1)}, bf16[1024,256]{1,0:T(8,128)(2,1)S(1)}, u32[]{:S(2)}, u32[]{:S(2)}) collective-permute-start(bf16[1024,256]{1,0:T(8,128)(2,1)S(1)} %slice.40), channel_id=1, source_target_pairs={{0,8},{1,9},{2,10},{3,11},{4,12},{5,13},{6,14},{7,15},{8,16},{9,17... | collective-permute-start | bytes 1572872 | tf_op jit(solution)/shard_map/ppermute | solution.py:38
  194.4 17.2 %collective-permute-start.25 = (bf16[1024,256]{1,0:T(8,128)(2,1)S(1)}, bf16[1024,256]{1,0:T(8,128)(2,1)S(1)}, u32[]{:S(2)}, u32[]{:S(2)}) collective-permute-start(bf16[1024,256]{1,0:T(8,128)(2,1)S(1)} %slice.41), channel_id=1, source_target_pairs={{0,56},{1,57},{2,58},{3,59},{4,60},{5,61},{6,62},{7,63},{8,0},{9,1... | collective-permute-start | bytes 1572872 | tf_op jit(solution)/shard_map/ppermute | solution.py:38
  204.1 9.8 %collective-permute-start.29 = (s16[272,256]{1,0:T(8,128)(2,1)S(1)}, s16[272,256]{1,0:T(8,128)(2,1)S(1)}, u32[]{:S(2)}, u32[]{:S(2)}) collective-permute-start(s16[272,256]{1,0:T(8,128)(2,1)S(1)} %get-tuple-element.161), channel_id=1, source_target_pairs={{0,7},{1,0},{2,1},{3,2},{4,3},{5,4},{6,5},{7,6},{8,15},{9,8},{10,9... | collective-permute-start | bytes 417800 | tf_op jit(solution)/shard_map/ppermute | solution.py:38
  204.3 13.2 %collective-permute-start.30 = (s16[272,256]{1,0:T(8,128)(2,1)S(1)}, s16[272,256]{1,0:T(8,128)(2,1)S(1)}, u32[]{:S(2)}, u32[]{:S(2)}) collective-permute-start(s16[272,256]{1,0:T(8,128)(2,1)S(1)} %get-tuple-element.162), channel_id=1, source_target_pairs={{0,6},{1,7},{2,0},{3,1},{4,2},{5,3},{6,4},{7,5},{8,14},{9,15},{10,... | collective-permute-start | bytes 417800 | tf_op jit(solution)/shard_map/ppermute | solution.py:38
  205.2 19.8 %collective-permute-start.31 = (s16[272,256]{1,0:T(8,128)(2,1)S(1)}, s16[272,256]{1,0:T(8,128)(2,1)S(1)}, u32[]{:S(2)}, u32[]{:S(2)}) collective-permute-start(s16[272,256]{1,0:T(8,128)(2,1)S(1)} %get-tuple-element.163), channel_id=1, source_target_pairs={{0,5},{1,6},{2,7},{3,0},{4,1},{5,2},{6,3},{7,4},{8,13},{9,14},{10,... | collective-permute-start | bytes 417800 | tf_op jit(solution)/shard_map/ppermute | solution.py:38
  208.7 16.2 %collective-permute-start.32 = (s16[272,256]{1,0:T(8,128)(2,1)S(1)}, s16[272,256]{1,0:T(8,128)(2,1)S(1)}, u32[]{:S(2)}, u32[]{:S(2)}) collective-permute-start(s16[272,256]{1,0:T(8,128)(2,1)S(1)} %get-tuple-element.164), channel_id=1, source_target_pairs={{0,4},{1,5},{2,6},{3,7},{4,0},{5,1},{6,2},{7,3},{8,12},{9,13},{10,... | collective-permute-start | bytes 417800 | tf_op jit(solution)/shard_map/ppermute | solution.py:38
  211.6 13.3 %collective-permute-start.33 = (s16[272,256]{1,0:T(8,128)(2,1)S(1)}, s16[272,256]{1,0:T(8,128)(2,1)S(1)}, u32[]{:S(2)}, u32[]{:S(2)}) collective-permute-start(s16[272,256]{1,0:T(8,128)(2,1)S(1)} %get-tuple-element.165), channel_id=1, source_target_pairs={{0,3},{1,4},{2,5},{3,6},{4,7},{5,0},{6,1},{7,2},{8,11},{9,12},{10,... | collective-permute-start | bytes 417800 | tf_op jit(solution)/shard_map/ppermute | solution.py:38
  213.9 11.9 %collective-permute-start.34 = (s16[272,256]{1,0:T(8,128)(2,1)S(1)}, s16[272,256]{1,0:T(8,128)(2,1)S(1)}, u32[]{:S(2)}, u32[]{:S(2)}) collective-permute-start(s16[272,256]{1,0:T(8,128)(2,1)S(1)} %get-tuple-element.166), channel_id=1, source_target_pairs={{0,2},{1,3},{2,4},{3,5},{4,6},{5,7},{6,0},{7,1},{8,10},{9,11},{10,... | collective-permute-start | bytes 417800 | tf_op jit(solution)/shard_map/ppermute | solution.py:38
  217.5 10.9 %collective-permute-start.35 = (s16[272,256]{1,0:T(8,128)(2,1)S(1)}, s16[272,256]{1,0:T(8,128)(2,1)S(1)}, u32[]{:S(2)}, u32[]{:S(2)}) collective-permute-start(s16[272,256]{1,0:T(8,128)(2,1)S(1)} %get-tuple-element.167), channel_id=1, source_target_pairs={{0,1},{1,2},{2,3},{3,4},{4,5},{5,6},{6,7},{7,0},{8,9},{9,10},{10,1... | collective-permute-start | bytes 417800 | tf_op jit(solution)/shard_map/ppermute | solution.py:38
  (10 other events, 62.6 us)
where the time goes:
time: 230 us; the launch traced here: 229 us
  waiting for transfers between devices  86.8 us (38%)
  starting transfers between devices  70.7 us (31%)
  Pallas kernels  62.8 us (27%)
  other arithmetic  4.24 us (2%)
  local copies, waits for them, and re-layouts  2.59 us (1%)
    ppermute x28, starting transfers between devices, send(): return lax.ppermute(x, GROUP, ring_pairs(side, step, bulk))  59 us
    ppermute x6, waiting for transfers between devices, exchange(): return lax.ppermute(x, GROUP, pairs)  51.5 us
    pallas_call x9, Pallas kernels, reduce_step(): pl.pallas_call(functools.partial(reduce_kernel, parts=len(weights), side=...  34 us
    ppermute x28, waiting for transfers between devices, send(): return lax.ppermute(x, GROUP, ring_pairs(side, step, bulk))  34 us
    pallas_call x5, Pallas kernels, gather_step(): pl.pallas_call(functools.partial(gather_kernel, parts=len(weights), side=...  27 us
    ppermute x6, starting transfers between devices, exchange(): return lax.ppermute(x, GROUP, pairs)  11.3 us
  transfers between devices with their start and end apart: 37, of which 13 were waited for; matrix products, arithmetic and copies ran while one was open for 3% of the time, Pallas kernels for 27%

commit v1 on v0

--- a/solution.py
+++ b/solution.py
@@ -9,7 +9,6 @@
 from jax.sharding import Mesh
 from jax.sharding import PartitionSpec as P
 
-MEMBERS = 4
 BLOCK = 128
 TENSOR = ("ty", "tx")
 GROUP = ("dp", "ty", "tx")
@@ -56,9 +55,9 @@
     return c, jnp.where(c == 0, y, x), jnp.where(c == 0, x, y)
 
 
-def start_weights(weights, buf, sem, side, slot, d, first, count):
+def start_weights(weights, buf, sem, side, lane, d, first, count):
     own, other = weights
-    n = buf.shape[2]
+    n = buf.shape[2] // sem.shape[0]
     here = own.shape[1] // n
     c, p, q = ring_place()
     chunk = lax.rem(p + (d + side), side)
@@ -68,15 +67,15 @@
         t = jnp.where(c == 0, side * chunk + piece, side * piece + chunk)
         half = (t >= here).astype(jnp.int32)
         at = pl.ds(pl.multiple_of((t - half * here) * n, n), n)
-        to = slot + k
+        to = buf.at[k, :, pl.ds(lane, n)]
 
         @pl.when(half == c)
         def _():
-            pltpu.make_async_copy(own.at[:, at], buf.at[to], sem.at[to]).start()
+            pltpu.make_async_copy(own.at[:, at], to, sem.at[lane // n, k]).start()
 
         @pl.when(half != c)
         def _():
-            pltpu.make_async_copy(other.at[:, at], buf.at[to], sem.at[to]).start()
+            pltpu.make_async_copy(other.at[:, at], to, sem.at[lane // n, k]).start()
 
         return 0
 
@@ -84,8 +83,11 @@
 
 
 def wait_weight(weights, buf, sem, slot):
-    n = buf.shape[2]
-    pltpu.make_async_copy(weights[0].at[:, pl.ds(0, n)], buf.at[slot], sem.at[slot]).wait()
+    n = buf.shape[2] // sem.shape[0]
+    for h in range(sem.shape[0]):
+        pltpu.make_async_copy(
+            weights[0].at[:, pl.ds(0, n)], buf.at[slot, :, pl.ds(h * n, n)], sem.at[h, slot]
+        ).wait()
 
 
 def coded(acc):
@@ -187,7 +189,7 @@
         scratch_shapes=([pltpu.VMEM(((count - 1) * (n + EXTRA), n), jnp.int16)] if last else [])
         + [
             pltpu.VMEM((count, width, n), masked.dtype),
-            pltpu.SemaphoreType.DMA((count,)),
+            pltpu.SemaphoreType.DMA((1, count)),
         ]
         + [pltpu.VMEM((EXTRA, n), jnp.float32) for _ in range(1 + len(recv))],
         compiler_params=PARAMS,
@@ -209,22 +211,19 @@
     n = acc.shape[1]
     each = held[0][2]
     for h, (d, first, count) in enumerate(held):
-        start_weights(weights, wbuf, sem, side, h * each, d, first, count)
+        start_weights(weights, wbuf, sem, side, h * n, d, first, count)
     total[...] = acc[...]
 
     def body(k, _):
         at = pl.ds(pl.multiple_of(k * n, n), n)
-        for h, x in enumerate(chunks):
-            wait_weight(weights, wbuf, sem, h * each + k)
-            total[...] += lax.dot_general(
-                wbuf[h * each + k],
-                x[at, :],
-                (((1,), (1,)), ((), ())),
-                preferred_element_type=jnp.float32,
-            )
+        wait_weight(weights, wbuf, sem, k)
+        rows = jnp.concatenate([x[at, :] for x in chunks], axis=1)
+        total[...] += lax.dot_general(
+            wbuf[k], rows, (((1,), (1,)), ((), ())), preferred_element_type=jnp.float32
+        )
         return 0
 
-    lax.fori_loop(0, each, body, 0, unroll=2 // len(held))
+    lax.fori_loop(0, each, body, 0, unroll=2)
     result = total[...]
     if last:
         result = live[...] * (result + adapter_scale * extra[...])
@@ -246,8 +245,8 @@
         out_specs=ALL_VMEM,
         scratch_shapes=[
             pltpu.VMEM(acc.shape, jnp.float32),
-            pltpu.VMEM((count, width, tokens), jnp.bfloat16),
-            pltpu.SemaphoreType.DMA((count,)),
+            pltpu.VMEM((count // len(held), width, tokens * len(held)), jnp.bfloat16),
+            pltpu.SemaphoreType.DMA((len(held), count // len(held))),
         ],
         compiler_params=PARAMS,
         cost_estimate=pl.CostEstimate(
@@ -278,16 +277,21 @@
     )(*map(vmem, (mine, extra, *parts)))
 
 
-def low_kernel(member_blocks, tokens, masked, own, other, sums, chosen):
+def low_kernel(member_blocks, tokens, masked, own, other, sums, chosen, table):
     each, rank, _ = own.shape
     n = tokens.shape[1]
     blocks = chosen.shape[0]
     c = lax.axis_index("dp").astype(jnp.int32)
+    row = lax.broadcasted_iota(jnp.int32, table.shape, 0)
+    lane = lax.broadcasted_iota(jnp.int32, table.shape, 1)
+    asked = jnp.where(row < each, c * each + row, (1 - c) * each + (row - each))
+    found = jnp.zeros(table.shape, jnp.float32)
     for b in range(blocks):
         end, member = jnp.int32(0), jnp.int32(0)
         for m in range(2 * each - 1):
             end = end + member_blocks[m]
             member = member + (end <= c * blocks + b).astype(jnp.int32)
+        found = jnp.where((lane == b) & (asked == member), 1.0, found)
         half = (member >= each).astype(jnp.int32)
         at = member - half * each
         factors = jnp.where(half == c, own[at], other[at])
@@ -297,6 +301,7 @@
             sums[rows, k * rank : (k + 1) * rank] = lax.dot_general(
                 x[rows, :], f, (((1,), (1,)), ((), ())), preferred_element_type=jnp.float32
             )
+    table[...] = found
 
 
 def low_parts(member_blocks, tokens, masked, own, other):
@@ -306,20 +311,15 @@
         out_shape=[
             pltpu.VMEM((tokens.shape[0], 2 * own.shape[1]), jnp.float32),
             pltpu.VMEM((blocks, *own.shape[1:]), own.dtype),
+            pltpu.VMEM((8, 128), jnp.float32),
         ],
         in_specs=[pl.BlockSpec(memory_space=pltpu.SMEM)] + [ALL_VMEM] * 4,
-        out_specs=[ALL_VMEM] * 2,
+        out_specs=[ALL_VMEM] * 3,
         compiler_params=PARAMS,
         cost_estimate=pl.CostEstimate(
             flops=2 * tokens.shape[0] * own[0].size, bytes_accessed=4 * own.size, transcendentals=0
         ),
     )(member_blocks, *map(vmem, (tokens, masked, own, other)))
-
-
-def block_members(member_blocks, first, count):
-    ends = jnp.cumsum(member_blocks)
-    blocks = first + jnp.arange(count, dtype=jnp.int32)
-    return jnp.sum((ends[None, :] <= blocks[:, None]).astype(jnp.int32), axis=1)
 
 
 def exchange(x, side, bit, bulk):
@@ -343,7 +343,6 @@
     token_rows, width_local = tokens.shape
     hidden_local = weight.shape[1]
     blocks_here = token_rows // BLOCK
-    c = lax.axis_index("dp").astype(jnp.int32)
     far = side // 2
 
     other = swap(weight.T)
@@ -367,21 +366,22 @@
         total, masked = tie(total, masked)
         return tie(gather_step(total, weights, chunks, held, side, extra), masked)
 
-    up, masked = reduce(masked, [], (), d=far, first=0, count=far)
-    down, masked = reduce(masked, [], (), d=-far, first=far, count=far)
-    up, down = send(up, side, 1, True), send(down, side, -1, True)
     below = jnp.concatenate([piece[0], piece[1]], axis=0)
     above = jnp.concatenate([piece[0], piece[side - 1]], axis=0)
     below, above = near(below, 2), near(above, -2)
+    up, masked = reduce(masked, [], (), d=far, first=0, count=far)
+    below, above, masked = tie(below, above, masked)
     piece[2], piece[3] = below[:token_rows], below[token_rows:]
     piece[side - 2], piece[side - 3] = above[:token_rows], above[token_rows:]
     piece[4] = near(piece[3], 1)
+    down, masked = reduce(masked, [], (), d=-far, first=far, count=far)
+    up, down = send(up, side, 1, True), send(down, side, -1, True)
     *pieces, masked = tie(*(piece[i] for i in range(side)), masked)
     home = jnp.concatenate(pieces, axis=0)
     ahead = send(home, side, 1, True)
     behind = send(home, side, -1, True)
 
-    sums, chosen = low_parts(member_blocks, tokens, masked, factors, other_factors)
+    sums, chosen, table = low_parts(member_blocks, tokens, masked, factors, other_factors)
     sums, masked = tie(sums, masked)
     rank = factors.shape[1]
     chosen_in, chosen_out = chosen[:, :, :width_local], chosen[:, :, width_local:]
@@ -454,15 +454,13 @@
     )
     up_outer = jnp.einsum("btr,btf->brf", low_in, grad_blocks, preferred_element_type=jnp.float32)
     outer = jnp.concatenate([down_outer, up_outer], axis=2)
-    members = block_members(member_blocks, c * blocks_here, blocks_here)
-    held_here = MEMBERS // 2
+    each = adapter_in.shape[0]
 
     def of_members(first):
-        owners = first + jnp.arange(held_here, dtype=jnp.int32)
-        picked = (owners[:, None] == members[None, :])[:, :, None, None]
-        return adapter_scale * jnp.where(picked, outer[None], 0.0).sum(axis=1)
-
-    grads = of_members(c * held_here) + swap(of_members((1 - c) * held_here))
+        share = table[first : first + each, :blocks_here, None, None]
+        return adapter_scale * (share * outer[None]).sum(axis=1)
+
+    grads = of_members(0) + swap(of_members(each))
     down_grad = grads[:, :, :width_local].transpose(0, 2, 1)
     return (hidden, input_gradient, down_grad, grads[:, :, width_local:])
 

time: 230 us -> 224 us (0.974)
  Pallas kernels: 62.8 us -> 52.9 us
  waiting for transfers between devices: 86.8 us -> 92.4 us
    ppermute x6, waiting for transfers between devices: 51.5 us -> 59.4 us  [exchange(): return lax.ppermute(x, GROUP, pairs)]
    pallas_call x5, Pallas kernels: 27 us -> 21.5 us  [gather_step(): pl.pallas_call(functools.partial(gather_kernel, parts=len(weights), side=...]
    pallas_call x9, Pallas kernels: 34 us -> 29.6 us  [reduce_step(): pl.pallas_call(functools.partial(reduce_kernel, parts=len(weights), side=...]
    ppermute x6, starting transfers between devices: 11.3 us -> 7.47 us  [exchange(): return lax.ppermute(x, GROUP, pairs)]
    ppermute x28, starting transfers between devices: 59 us -> 62.4 us  [send(): return lax.ppermute(x, GROUP, ring_pairs(side, step, bulk))]
    ppermute x28, waiting for transfers between devices: 34 us -> 31.6 us  [send(): return lax.ppermute(x, GROUP, ring_pairs(side, step, bulk))]
  transfers between devices with their start and end apart: 37 -> 37, of which waited for: 13 -> 17; matrix products, arithmetic and copies ran while one was open for 3% -> 2% of each run, Pallas kernels for 27% -> 23%
where the time goes in v1:
time: 224 us; the launch traced here: 222 us
  waiting for transfers between devices  92.4 us (41%)
  starting transfers between devices  70.3 us (31%)
  Pallas kernels  52.9 us (24%)
  local copies, waits for them, and re-layouts  2.59 us (1%)
    ppermute x28, starting transfers between devices, send(): return lax.ppermute(x, GROUP, ring_pairs(side, step, bulk))  62.4 us
    ppermute x6, waiting for transfers between devices, exchange(): return lax.ppermute(x, GROUP, pairs)  59.4 us
    ppermute x28, waiting for transfers between devices, send(): return lax.ppermute(x, GROUP, ring_pairs(side, step, bulk))  31.6 us
    pallas_call x9, Pallas kernels, reduce_step(): pl.pallas_call(functools.partial(reduce_kernel, parts=len(weights), side=...  29.6 us
    pallas_call x5, Pallas kernels, gather_step(): pl.pallas_call(functools.partial(gather_kernel, parts=len(weights), side=...  21.5 us
    ppermute x6, starting transfers between devices, exchange(): return lax.ppermute(x, GROUP, pairs)  7.47 us
  transfers between devices with their start and end apart: 37, of which 17 were waited for; matrix products, arithmetic and copies ran while one was open for 2% of the time, Pallas kernels for 23%

profile of v1, /device:TPU:518, one launch (start us, length us, event | category | flops | bytes accessed | tf_op | source)
XLA Modules:
  0.0 222.4 jit_solution(16941932983022049892)
XLA Ops:
  1.3 2.8 %collective-permute-start = (bf16[256,256]{1,0:T(8,128)(2,1)}, bf16[256,256]{1,0:T(8,128)(2,1)S(1)}, u32[]{:S(2)}, u32[]{:S(2)}) collective-permute-start(bf16[256,256]{1,0:T(8,128)(2,1)} %tokens.1), channel_id=1, source_target_pairs={{0,1},{1,2},{2,3},{3,4},{4,5},{5,6},{6,7},{7,0},{8,9},{9,10},{10,1... | collective-permute-start | bytes 393224 | tf_op jit(solution)/shard_map/ppermute | solution.py:37
  4.1 3.2 %collective-permute-done.2 = bf16[256,256]{1,0:T(8,128)(2,1)S(1)} collective-permute-done((bf16[256,256]{1,0:T(8,128)(2,1)}, bf16[256,256]{1,0:T(8,128)(2,1)S(1)}, u32[]{:S(2)}, u32[]{:S(2)}) %collective-permute-start.2) | collective-permute-done | bytes 131104 | tf_op jit(solution)/shard_map/ppermute | solution.py:37
  8.2 18.5 %collective-permute-start.3 = (bf16[512,256]{1,0:T(8,128)(2,1)S(1)}, bf16[512,256]{1,0:T(8,128)(2,1)S(1)}, u32[]{:S(2)}, u32[]{:S(2)}) collective-permute-start(bf16[512,256]{1,0:T(8,128)(2,1)S(1)} %get-tuple-element.182), channel_id=1, source_target_pairs={{0,6},{1,7},{2,0},{3,1},{4,2},{5,3},{6,4},{7,5},{8,14},{9,15},{10,... | collective-permute-start | bytes 786440 | tf_op jit(solution)/shard_map/ppermute | solution.py:37
  30.1 3.3 %collective-permute-done.3 = bf16[512,256]{1,0:T(8,128)(2,1)S(1)} collective-permute-done((bf16[512,256]{1,0:T(8,128)(2,1)S(1)}, bf16[512,256]{1,0:T(8,128)(2,1)S(1)}, u32[]{:S(2)}, u32[]{:S(2)}) %collective-permute-start.3) | collective-permute-done | bytes 262176 | tf_op jit(solution)/shard_map/ppermute | solution.py:37
  33.5 3.4 %collective-permute-done.1 = bf16[512,256]{1,0:T(8,128)(2,1)S(1)} collective-permute-done((bf16[512,256]{1,0:T(8,128)(2,1)S(1)}, bf16[512,256]{1,0:T(8,128)(2,1)S(1)}, u32[]{:S(2)}, u32[]{:S(2)}) %collective-permute-start.1) | collective-permute-done | bytes 262176 | tf_op jit(solution)/shard_map/ppermute | solution.py:37
  45.7 3.2 %collective-permute-start.11 = (s16[1040,256]{1,0:T(8,128)(2,1)S(1)}, s16[1040,256]{1,0:T(8,128)(2,1)S(1)}, u32[]{:S(2)}, u32[]{:S(2)}) collective-permute-start(s16[1040,256]{1,0:T(8,128)(2,1)S(1)} %shard_map.103), channel_id=1, source_target_pairs={{0,56},{1,57},{2,58},{3,59},{4,60},{5,61},{6,62},{7,63},{8,0},{9,1... | collective-permute-start | bytes 1597448 | tf_op jit(solution)/shard_map/ppermute | solution.py:37
  51.4 3.4 %shard_map.105.acc = f32[416,256]{1,0:T(8,128)S(1)} custom-call(f32[416,256]{1,0:T(8,128)S(1)} %broadcast_in_dim.2.acc, bf16[416,8192]{1,0:T(8,128)(2,1)} %bitcast.34, bf16[416,8192]{1,0:T(8,128)(2,1)} %collective-permute-done.4.refs_1_, bf16[2048,256]{1,0:T(8,128)(2,1)S(1)} %constant_dynamic-update-slice_fusion.refs_2_), custom_call_target="tpu_custom_call" | custom-call | flops 436207616 | bytes 2752512 | tf_op jit(solution)/shard_map/pallas_call | solution.py:237
  54.8 10.7 %collective-permute-done.10.refs_2_ = s16[1040,256]{1,0:T(8,128)(2,1)S(1)} collective-permute-done((s16[1040,256]{1,0:T(8,128)(2,1)S(1)}, s16[1040,256]{1,0:T(8,128)(2,1)S(1)}, u32[]{:S(2)}, u32[]{:S(2)}) %collective-permute-start.10) | collective-permute-done | bytes 532512 | tf_op jit(solution)/shard_map/ppermute | solution.py:37
  65.5 3.2 %shard_map.106 = s16[2064,256]{1,0:T(8,128)(2,1)S(1)} custom-call(bf16[256,416]{1,0:T(8,128)(2,1)S(1)} %broadcast_multiply_fusion.1.m.masked, bf16[416,8192]{1,0:T(8,128)(2,1)} %bitcast.35, bf16[416,8192]{1,0:T(8,128)(2,1)} %collective-permute-done.4.refs_1_, s16[1040,256]{1,0:T(8,128)(2,1)S(1)} %collective-permute-done.10.refs_2_), custom_call_target="tpu_custom_call" | custom-call | flops 436207616 | bytes 3801088 | tf_op jit(solution)/shard_map/pallas_call | solution.py:175
  69.5 3.3 %shard_map.107 = s16[2064,256]{1,0:T(8,128)(2,1)S(1)} custom-call(bf16[256,416]{1,0:T(8,128)(2,1)S(1)} %broadcast_multiply_fusion.1.m.masked, bf16[416,8192]{1,0:T(8,128)(2,1)} %bitcast.36, bf16[416,8192]{1,0:T(8,128)(2,1)} %collective-permute-done.4.refs_1_, s16[1040,256]{1,0:T(8,128)(2,1)S(1)} %collective-permute-done.11.refs_2_), custom_call_target="tpu_custom_call" | custom-call | flops 436207616 | bytes 3801088 | tf_op jit(solution)/shard_map/pallas_call | solution.py:175
  72.8 2.8 %collective-permute-start.17 = (s16[2064,256]{1,0:T(8,128)(2,1)S(1)}, s16[2064,256]{1,0:T(8,128)(2,1)S(1)}, u32[]{:S(2)}, u32[]{:S(2)}) collective-permute-start(s16[2064,256]{1,0:T(8,128)(2,1)S(1)} %shard_map.107), channel_id=1, source_target_pairs={{0,56},{1,57},{2,58},{3,59},{4,60},{5,61},{6,62},{7,63},{8,0},{9,1... | collective-permute-start | bytes 3170312 | tf_op jit(solution)/shard_map/ppermute | solution.py:37
  75.7 3.2 %collective-permute-start.15 = (bf16[2048,256]{1,0:T(8,128)(2,1)S(1)}, bf16[2048,256]{1,0:T(8,128)(2,1)S(1)}, u32[]{:S(2)}, u32[]{:S(2)}) collective-permute-start(bf16[2048,256]{1,0:T(8,128)(2,1)S(1)} %collective-permute-done.9.refs_3_), channel_id=1, source_target_pairs={{0,56},{1,57},{2,58},{3,59},{4,60},{5,61},{6,62},{7,63},{8,0},{9,1... | collective-permute-start | bytes 3145736 | tf_op jit(solution)/shard_map/ppermute | solution.py:37
  78.9 23.2 %collective-permute-done.7 = f32[256,128]{1,0:T(8,128)S(1)} collective-permute-done((f32[256,128]{1,0:T(8,128)S(1)}, f32[256,128]{1,0:T(8,128)S(1)}, u32[]{:S(2)}, u32[]{:S(2)}) %collective-permute-start.7) | collective-permute-done | bytes 131104 | tf_op jit(solution)/shard_map/ppermute | solution.py:335
  102.2 5.0 %shard_map.108.acc = f32[416,256]{1,0:T(8,128)S(1)} custom-call(f32[416,256]{1,0:T(8,128)S(1)} %shard_map.105.acc, bf16[416,8192]{1,0:T(8,128)(2,1)} %bitcast.37, bf16[416,8192]{1,0:T(8,128)(2,1)} %collective-permute-done.4.refs_1_, bf16[2048,256]{1,0:T(8,128)(2,1)S(1)} %collective-permute-done.8.refs_2_, bf16[2048,256]{1,0:T(8,128)(2,1)S(1)} %collective-permute-done.9.refs_3_), custom_call_target="tpu_custom_call" | custom-call | flops 872415232 | bytes 5505024 | tf_op jit(solution)/shard_map/pallas_call | solution.py:237
  108.6 3.8 %shard_map.109 = s16[2064,256]{1,0:T(8,128)(2,1)S(1)} custom-call(bf16[256,416]{1,0:T(8,128)(2,1)S(1)} %broadcast_multiply_fusion.1.m.masked, bf16[416,8192]{1,0:T(8,128)(2,1)} %bitcast.38, bf16[416,8192]{1,0:T(8,128)(2,1)} %collective-permute-done.4.refs_1_, s16[2064,256]{1,0:T(8,128)(2,1)S(1)} %collective-permute-done.16.refs_2_), custom_call_target="tpu_custom_call" | custom-call | flops 436207616 | bytes 3801088 | tf_op jit(solution)/shard_map/pallas_call | solution.py:175
  112.5 3.8 %shard_map.110 = s16[2064,256]{1,0:T(8,128)(2,1)S(1)} custom-call(bf16[256,416]{1,0:T(8,128)(2,1)S(1)} %broadcast_multiply_fusion.1.m.masked, bf16[416,8192]{1,0:T(8,128)(2,1)} %bitcast.39, bf16[416,8192]{1,0:T(8,128)(2,1)} %collective-permute-done.4.refs_1_, s16[2064,256]{1,0:T(8,128)(2,1)S(1)} %collective-permute-done.17.refs_2_), custom_call_target="tpu_custom_call" | custom-call | flops 436207616 | bytes 3801088 | tf_op jit(solution)/shard_map/pallas_call | solution.py:175
  116.3 3.3 %collective-permute-start.23 = (s16[2064,256]{1,0:T(8,128)(2,1)S(1)}, s16[2064,256]{1,0:T(8,128)(2,1)S(1)}, u32[]{:S(2)}, u32[]{:S(2)}) collective-permute-start(s16[2064,256]{1,0:T(8,128)(2,1)S(1)} %shard_map.110), channel_id=1, source_target_pairs={{0,56},{1,57},{2,58},{3,59},{4,60},{5,61},{6,62},{7,63},{8,0},{9,1... | collective-permute-start | bytes 3170312 | tf_op jit(solution)/shard_map/ppermute | solution.py:37
  119.6 3.2 %collective-permute-start.21 = (bf16[2048,256]{1,0:T(8,128)(2,1)S(1)}, bf16[2048,256]{1,0:T(8,128)(2,1)S(1)}, u32[]{:S(2)}, u32[]{:S(2)}) collective-permute-start(bf16[2048,256]{1,0:T(8,128)(2,1)S(1)} %collective-permute-done.15.refs_3_), channel_id=1, source_target_pairs={{0,56},{1,57},{2,58},{3,59},{4,60},{5,61},{6,62},{7,63},{8,0},{9,1... | collective-permute-start | bytes 3145736 | tf_op jit(solution)/shard_map/ppermute | solution.py:37
  122.8 24.1 %collective-permute-done.13 = f32[256,128]{1,0:T(8,128)S(1)} collective-permute-done((f32[256,128]{1,0:T(8,128)S(1)}, f32[256,128]{1,0:T(8,128)S(1)}, u32[]{:S(2)}, u32[]{:S(2)}) %collective-permute-start.13) | collective-permute-done | bytes 131104 | tf_op jit(solution)/shard_map/ppermute | solution.py:335
  147.1 5.0 %shard_map.111.acc = f32[416,256]{1,0:T(8,128)S(1)} custom-call(f32[416,256]{1,0:T(8,128)S(1)} %shard_map.108.acc, bf16[416,8192]{1,0:T(8,128)(2,1)} %bitcast.40, bf16[416,8192]{1,0:T(8,128)(2,1)} %collective-permute-done.4.refs_1_, bf16[2048,256]{1,0:T(8,128)(2,1)S(1)} %collective-permute-done.14.refs_2_, bf16[2048,256]{1,0:T(8,128)(2,1)S(1)} %collective-permute-done.15.refs_3_), custom_call_target="tpu_custom_call" | custom-call | flops 872415232 | bytes 5505024 | tf_op jit(solution)/shard_map/pallas_call | solution.py:237
  152.1 3.6 %collective-permute-done.18 = f32[256,128]{1,0:T(8,128)S(1)} collective-permute-done((f32[256,128]{1,0:T(8,128)S(1)}, f32[256,128]{1,0:T(8,128)S(1)}, u32[]{:S(2)}, u32[]{:S(2)}) %collective-permute-start.18) | collective-permute-done | bytes 131104 | tf_op jit(solution)/shard_map/ppermute | solution.py:335
  155.7 5.5 %collective-permute-start.19 = (f32[256,128]{1,0:T(8,128)S(1)}, f32[256,128]{1,0:T(8,128)S(1)}, u32[]{:S(2)}, u32[]{:S(2)}) collective-permute-start(f32[256,128]{1,0:T(8,128)S(1)} %add.24), channel_id=1, source_target_pairs={{0,32},{1,33},{2,34},{3,35},{4,36},{5,37},{6,38},{7,39},{8,40},{9,... | collective-permute-start | bytes 393224 | tf_op jit(solution)/shard_map/ppermute | solution.py:335
  161.3 7.3 %collective-permute-done.19 = f32[256,128]{1,0:T(8,128)S(1)} collective-permute-done((f32[256,128]{1,0:T(8,128)S(1)}, f32[256,128]{1,0:T(8,128)S(1)}, u32[]{:S(2)}, u32[]{:S(2)}) %collective-permute-start.19) | collective-permute-done | bytes 131104 | tf_op jit(solution)/shard_map/ppermute | solution.py:335
  168.6 3.8 %shard_map.112 = s16[2064,256]{1,0:T(8,128)(2,1)S(1)} custom-call(bf16[256,416]{1,0:T(8,128)(2,1)S(1)} %broadcast_multiply_fusion.1.m.masked, bf16[416,8192]{1,0:T(8,128)(2,1)} %bitcast.41, bf16[416,8192]{1,0:T(8,128)(2,1)} %collective-permute-done.4.refs_1_, s16[2064,256]{1,0:T(8,128)(2,1)S(1)} %collective-permute-done.22.refs_2_), custom_call_target="tpu_custom_call" | custom-call | flops 436207616 | bytes 3801088 | tf_op jit(solution)/shard_map/pallas_call | solution.py:175
  172.4 3.8 %shard_map.113 = s16[2064,256]{1,0:T(8,128)(2,1)S(1)} custom-call(bf16[256,416]{1,0:T(8,128)(2,1)S(1)} %broadcast_multiply_fusion.1.m.masked, bf16[416,8192]{1,0:T(8,128)(2,1)} %bitcast.42, bf16[416,8192]{1,0:T(8,128)(2,1)} %collective-permute-done.4.refs_1_, s16[2064,256]{1,0:T(8,128)(2,1)S(1)} %collective-permute-done.23.refs_2_), custom_call_target="tpu_custom_call" | custom-call | flops 436207616 | bytes 3801088 | tf_op jit(solution)/shard_map/pallas_call | solution.py:175
  179.9 5.0 %shard_map.114.acc = f32[416,256]{1,0:T(8,128)S(1)} custom-call(f32[416,256]{1,0:T(8,128)S(1)} %shard_map.111.acc, bf16[416,8192]{1,0:T(8,128)(2,1)} %bitcast.43, bf16[416,8192]{1,0:T(8,128)(2,1)} %collective-permute-done.4.refs_1_, bf16[2048,256]{1,0:T(8,128)(2,1)S(1)} %collective-permute-done.20.refs_2_, bf16[2048,256]{1,0:T(8,128)(2,1)S(1)} %collective-permute-done.21.refs_3_), custom_call_target="tpu_custom_call" | custom-call | flops 872415232 | bytes 5505024 | tf_op jit(solution)/shard_map/pallas_call | solution.py:237
  185.1 3.2 %collective-permute-start.25 = (bf16[1024,256]{1,0:T(8,128)(2,1)S(1)}, bf16[1024,256]{1,0:T(8,128)(2,1)S(1)}, u32[]{:S(2)}, u32[]{:S(2)}) collective-permute-start(bf16[1024,256]{1,0:T(8,128)(2,1)S(1)} %slice.47), channel_id=1, source_target_pairs={{0,56},{1,57},{2,58},{3,59},{4,60},{5,61},{6,62},{7,63},{8,0},{9,1... | collective-permute-start | bytes 1572872 | tf_op jit(solution)/shard_map/ppermute | solution.py:37
  189.7 2.9 %collective-permute-done.28.refs_3_ = s16[2064,256]{1,0:T(8,128)(2,1)S(1)} collective-permute-done((s16[2064,256]{1,0:T(8,128)(2,1)S(1)}, s16[2064,256]{1,0:T(8,128)(2,1)S(1)}, u32[]{:S(2)}, u32[]{:S(2)}) %collective-permute-start.28) | collective-permute-done | bytes 1056800 | tf_op jit(solution)/shard_map/ppermute | solution.py:37
  193.9 3.3 %shard_map.116 = (f32[256,256]{1,0:T(8,128)S(1)}, s16[272,256]{1,0:T(8,128)(2,1)S(1)}, s16[272,256]{1,0:T(8,128)(2,1)S(1)}, s16[272,256]{1,0:T(8,128)(2,1)S(1)},...) custom-call(bf16[256,416]{1,0:T(8,128)(2,1)S(1)} %broadcast_multiply, ...), custom_call_target="tpu_custom_call" | custom-call | flops 436207616 | bytes 3801088 | tf_op jit(solution)/shard_map/pallas_call | solution.py:175
  197.9 4.4 %collective-permute-start.31 = (s16[272,256]{1,0:T(8,128)(2,1)S(1)}, s16[272,256]{1,0:T(8,128)(2,1)S(1)}, u32[]{:S(2)}, u32[]{:S(2)}) collective-permute-start(s16[272,256]{1,0:T(8,128)(2,1)S(1)} %get-tuple-element.170), channel_id=1, source_target_pairs={{0,5},{1,6},{2,7},{3,0},{4,1},{5,2},{6,3},{7,4},{8,13},{9,14},{10,... | collective-permute-start | bytes 417800 | tf_op jit(solution)/shard_map/ppermute | solution.py:37
  207.5 3.7 %collective-permute-start.34 = (s16[272,256]{1,0:T(8,128)(2,1)S(1)}, s16[272,256]{1,0:T(8,128)(2,1)S(1)}, u32[]{:S(2)}, u32[]{:S(2)}) collective-permute-start(s16[272,256]{1,0:T(8,128)(2,1)S(1)} %get-tuple-element.173), channel_id=1, source_target_pairs={{0,2},{1,3},{2,4},{3,5},{4,6},{5,7},{6,0},{7,1},{8,10},{9,11},{10,... | collective-permute-start | bytes 417800 | tf_op jit(solution)/shard_map/ppermute | solution.py:37
  214.5 3.1 %shard_map.115 = bf16[416,256]{1,0:T(8,128)(2,1)S(1)} custom-call(f32[416,256]{1,0:T(8,128)S(1)} %shard_map.114.acc, bf16[416,8192]{1,0:T(8,128)(2,1)} %bitcast.45, bf16[416,8192]{1,0:T(8,128)(2,1)} %collective-permute-done.4.refs_1_, bf16[1024,256]{1,0:T(8,128)(2,1)S(1)} %collective-permute-done.24.refs_2_, ...), custom_call_target="tpu_custom_call" | custom-call | flops 436207616 | bytes 2752512 | tf_op jit(solution)/shard_map/pallas_call | solution.py:237
  (106 shorter events, 39.3 us)
Async XLA Ops:
  0.6 27.1 %collective-permute-start.4 = (bf16[416,8192]{1,0:T(8,128)(2,1)}, bf16[416,8192]{1,0:T(8,128)(2,1)}, u32[]{:S(2)}, u32[]{:S(2)}) collective-permute-start(bf16[416,8192]{1,0:T(8,128)(2,1)} %bitcast.31), channel_id=1, source_target_pairs={{0,64},{64,0},{1,65},{65,1},{2,66},{66,2},{3,67},{67,3},{4,68},{68... | collective-permute-start | bytes 20447240 | tf_op jit(solution)/shard_map/ppermute | solution.py:41
  8.2 25.2 %collective-permute-start.3 = (bf16[512,256]{1,0:T(8,128)(2,1)S(1)}, bf16[512,256]{1,0:T(8,128)(2,1)S(1)}, u32[]{:S(2)}, u32[]{:S(2)}) collective-permute-start(bf16[512,256]{1,0:T(8,128)(2,1)S(1)} %get-tuple-element.182), channel_id=1, source_target_pairs={{0,6},{1,7},{2,0},{3,1},{4,2},{5,3},{6,4},{7,5},{8,14},{9,15},{10,... | collective-permute-start | bytes 786440 | tf_op jit(solution)/shard_map/ppermute | solution.py:37
  26.8 10.1 %collective-permute-start.1 = (bf16[512,256]{1,0:T(8,128)(2,1)S(1)}, bf16[512,256]{1,0:T(8,128)(2,1)S(1)}, u32[]{:S(2)}, u32[]{:S(2)}) collective-permute-start(bf16[512,256]{1,0:T(8,128)(2,1)S(1)} %get-tuple-element.183), channel_id=1, source_target_pairs={{0,2},{1,3},{2,4},{3,5},{4,6},{5,7},{6,0},{7,1},{8,10},{9,11},{10,... | collective-permute-start | bytes 786440 | tf_op jit(solution)/shard_map/ppermute | solution.py:37
  43.5 32.1 %collective-permute-start.9 = (bf16[2048,256]{1,0:T(8,128)(2,1)S(1)}, bf16[2048,256]{1,0:T(8,128)(2,1)S(1)}, u32[]{:S(2)}, u32[]{:S(2)}) collective-permute-start(bf16[2048,256]{1,0:T(8,128)(2,1)S(1)} %constant_dynamic-update-slice_fusion.refs_2_), channel_id=1, source_target_pairs={{0,56},{1,57},{2,58},{3,59},{4,60},{5,61},{6,62},{7,63},{8,0},{9,1... | collective-permute-start | bytes 3145736 | tf_op jit(solution)/shard_map/ppermute | solution.py:37
  43.7 32.0 %collective-permute-start.8 = (bf16[2048,256]{1,0:T(8,128)(2,1)S(1)}, bf16[2048,256]{1,0:T(8,128)(2,1)S(1)}, u32[]{:S(2)}, u32[]{:S(2)}) collective-permute-start(bf16[2048,256]{1,0:T(8,128)(2,1)S(1)} %constant_dynamic-update-slice_fusion.refs_2_), channel_id=1, source_target_pairs={{0,8},{1,9},{2,10},{3,11},{4,12},{5,13},{6,14},{7,15},{8,16},{9,17... | collective-permute-start | bytes 3145736 | tf_op jit(solution)/shard_map/ppermute | solution.py:37
  45.7 19.8 %collective-permute-start.10 = (s16[1040,256]{1,0:T(8,128)(2,1)S(1)}, s16[1040,256]{1,0:T(8,128)(2,1)S(1)}, u32[]{:S(2)}, u32[]{:S(2)}) collective-permute-start(s16[1040,256]{1,0:T(8,128)(2,1)S(1)} %shard_map.102), channel_id=1, source_target_pairs={{0,8},{1,9},{2,10},{3,11},{4,12},{5,13},{6,14},{7,15},{8,16},{9,17... | collective-permute-start | bytes 1597448 | tf_op jit(solution)/shard_map/ppermute | solution.py:37
  45.7 23.9 %collective-permute-start.11 = (s16[1040,256]{1,0:T(8,128)(2,1)S(1)}, s16[1040,256]{1,0:T(8,128)(2,1)S(1)}, u32[]{:S(2)}, u32[]{:S(2)}) collective-permute-start(s16[1040,256]{1,0:T(8,128)(2,1)S(1)} %shard_map.103), channel_id=1, source_target_pairs={{0,56},{1,57},{2,58},{3,59},{4,60},{5,61},{6,62},{7,63},{8,0},{9,1... | collective-permute-start | bytes 1597448 | tf_op jit(solution)/shard_map/ppermute | solution.py:37
  68.7 39.8 %collective-permute-start.16 = (s16[2064,256]{1,0:T(8,128)(2,1)S(1)}, s16[2064,256]{1,0:T(8,128)(2,1)S(1)}, u32[]{:S(2)}, u32[]{:S(2)}) collective-permute-start(s16[2064,256]{1,0:T(8,128)(2,1)S(1)} %shard_map.106), channel_id=1, source_target_pairs={{0,8},{1,9},{2,10},{3,11},{4,12},{5,13},{6,14},{7,15},{8,16},{9,17... | collective-permute-start | bytes 3170312 | tf_op jit(solution)/shard_map/ppermute | solution.py:37
  72.8 39.7 %collective-permute-start.17 = (s16[2064,256]{1,0:T(8,128)(2,1)S(1)}, s16[2064,256]{1,0:T(8,128)(2,1)S(1)}, u32[]{:S(2)}, u32[]{:S(2)}) collective-permute-start(s16[2064,256]{1,0:T(8,128)(2,1)S(1)} %shard_map.107), channel_id=1, source_target_pairs={{0,56},{1,57},{2,58},{3,59},{4,60},{5,61},{6,62},{7,63},{8,0},{9,1... | collective-permute-start | bytes 3170312 | tf_op jit(solution)/shard_map/ppermute | solution.py:37
  75.6 43.9 %collective-permute-start.14 = (bf16[2048,256]{1,0:T(8,128)(2,1)S(1)}, bf16[2048,256]{1,0:T(8,128)(2,1)S(1)}, u32[]{:S(2)}, u32[]{:S(2)}) collective-permute-start(bf16[2048,256]{1,0:T(8,128)(2,1)S(1)} %collective-permute-done.8.refs_2_), channel_id=1, source_target_pairs={{0,8},{1,9},{2,10},{3,11},{4,12},{5,13},{6,14},{7,15},{8,16},{9,17... | collective-permute-start | bytes 3145736 | tf_op jit(solution)/shard_map/ppermute | solution.py:37
  75.7 43.9 %collective-permute-start.15 = (bf16[2048,256]{1,0:T(8,128)(2,1)S(1)}, bf16[2048,256]{1,0:T(8,128)(2,1)S(1)}, u32[]{:S(2)}, u32[]{:S(2)}) collective-permute-start(bf16[2048,256]{1,0:T(8,128)(2,1)S(1)} %collective-permute-done.9.refs_3_), channel_id=1, source_target_pairs={{0,56},{1,57},{2,58},{3,59},{4,60},{5,61},{6,62},{7,63},{8,0},{9,1... | collective-permute-start | bytes 3145736 | tf_op jit(solution)/shard_map/ppermute | solution.py:37
  78.9 23.2 %collective-permute-start.7 = (f32[256,128]{1,0:T(8,128)S(1)}, f32[256,128]{1,0:T(8,128)S(1)}, u32[]{:S(2)}, u32[]{:S(2)}) collective-permute-start(f32[256,128]{1,0:T(8,128)S(1)} %get-tuple-element.109), channel_id=1, source_target_pairs={{0,8},{1,9},{2,10},{3,11},{4,12},{5,13},{6,14},{7,15},{8,0},{9,1},... | collective-permute-start | bytes 393224 | tf_op jit(solution)/shard_map/ppermute | solution.py:335
  112.4 56.2 %collective-permute-start.22 = (s16[2064,256]{1,0:T(8,128)(2,1)S(1)}, s16[2064,256]{1,0:T(8,128)(2,1)S(1)}, u32[]{:S(2)}, u32[]{:S(2)}) collective-permute-start(s16[2064,256]{1,0:T(8,128)(2,1)S(1)} %shard_map.109), channel_id=1, source_target_pairs={{0,8},{1,9},{2,10},{3,11},{4,12},{5,13},{6,14},{7,15},{8,16},{9,17... | collective-permute-start | bytes 3170312 | tf_op jit(solution)/shard_map/ppermute | solution.py:37
  116.3 56.1 %collective-permute-start.23 = (s16[2064,256]{1,0:T(8,128)(2,1)S(1)}, s16[2064,256]{1,0:T(8,128)(2,1)S(1)}, u32[]{:S(2)}, u32[]{:S(2)}) collective-permute-start(s16[2064,256]{1,0:T(8,128)(2,1)S(1)} %shard_map.110), channel_id=1, source_target_pairs={{0,56},{1,57},{2,58},{3,59},{4,60},{5,61},{6,62},{7,63},{8,0},{9,1... | collective-permute-start | bytes 3170312 | tf_op jit(solution)/shard_map/ppermute | solution.py:37
  119.6 56.6 %collective-permute-start.20 = (bf16[2048,256]{1,0:T(8,128)(2,1)S(1)}, bf16[2048,256]{1,0:T(8,128)(2,1)S(1)}, u32[]{:S(2)}, u32[]{:S(2)}) collective-permute-start(bf16[2048,256]{1,0:T(8,128)(2,1)S(1)} %collective-permute-done.14.refs_2_), channel_id=1, source_target_pairs={{0,8},{1,9},{2,10},{3,11},{4,12},{5,13},{6,14},{7,15},{8,16},{9,17... | collective-permute-start | bytes 3145736 | tf_op jit(solution)/shard_map/ppermute | solution.py:37
  119.6 56.6 %collective-permute-start.21 = (bf16[2048,256]{1,0:T(8,128)(2,1)S(1)}, bf16[2048,256]{1,0:T(8,128)(2,1)S(1)}, u32[]{:S(2)}, u32[]{:S(2)}) collective-permute-start(bf16[2048,256]{1,0:T(8,128)(2,1)S(1)} %collective-permute-done.15.refs_3_), channel_id=1, source_target_pairs={{0,56},{1,57},{2,58},{3,59},{4,60},{5,61},{6,62},{7,63},{8,0},{9,1... | collective-permute-start | bytes 3145736 | tf_op jit(solution)/shard_map/ppermute | solution.py:37
  122.8 24.1 %collective-permute-start.13 = (f32[256,128]{1,0:T(8,128)S(1)}, f32[256,128]{1,0:T(8,128)S(1)}, u32[]{:S(2)}, u32[]{:S(2)}) collective-permute-start(f32[256,128]{1,0:T(8,128)S(1)} %add.22), channel_id=1, source_target_pairs={{0,16},{1,17},{2,18},{3,19},{4,20},{5,21},{6,22},{7,23},{8,24},{9,... | collective-permute-start | bytes 393224 | tf_op jit(solution)/shard_map/ppermute | solution.py:335
  146.9 8.8 %collective-permute-start.18 = (f32[256,128]{1,0:T(8,128)S(1)}, f32[256,128]{1,0:T(8,128)S(1)}, u32[]{:S(2)}, u32[]{:S(2)}) collective-permute-start(f32[256,128]{1,0:T(8,128)S(1)} %add.23), channel_id=1, source_target_pairs={{0,2},{1,3},{2,0},{3,1},{4,6},{5,7},{6,4},{7,5},{8,10},{9,11},{10,... | collective-permute-start | bytes 393224 | tf_op jit(solution)/shard_map/ppermute | solution.py:335
  155.7 12.8 %collective-permute-start.19 = (f32[256,128]{1,0:T(8,128)S(1)}, f32[256,128]{1,0:T(8,128)S(1)}, u32[]{:S(2)}, u32[]{:S(2)}) collective-permute-start(f32[256,128]{1,0:T(8,128)S(1)} %add.24), channel_id=1, source_target_pairs={{0,32},{1,33},{2,34},{3,35},{4,36},{5,37},{6,38},{7,39},{8,40},{9,... | collective-permute-start | bytes 393224 | tf_op jit(solution)/shard_map/ppermute | solution.py:335
  176.2 12.1 %collective-permute-start.26 = (f32[256,128]{1,0:T(8,128)S(1)}, f32[256,128]{1,0:T(8,128)S(1)}, u32[]{:S(2)}, u32[]{:S(2)}) collective-permute-start(f32[256,128]{1,0:T(8,128)S(1)} %add.25), channel_id=1, source_target_pairs={{0,4},{1,5},{2,6},{3,7},{4,0},{5,1},{6,2},{7,3},{8,12},{9,13},{10,... | collective-permute-start | bytes 393224 | tf_op jit(solution)/shard_map/ppermute | solution.py:335
  177.8 14.9 %collective-permute-start.28 = (s16[2064,256]{1,0:T(8,128)(2,1)S(1)}, s16[2064,256]{1,0:T(8,128)(2,1)S(1)}, u32[]{:S(2)}, u32[]{:S(2)}) collective-permute-start(s16[2064,256]{1,0:T(8,128)(2,1)S(1)} %shard_map.113), channel_id=1, source_target_pairs={{0,56},{1,57},{2,58},{3,59},{4,60},{5,61},{6,62},{7,63},{8,0},{9,1... | collective-permute-start | bytes 3170312 | tf_op jit(solution)/shard_map/ppermute | solution.py:37
  177.8 16.1 %collective-permute-start.27 = (s16[2064,256]{1,0:T(8,128)(2,1)S(1)}, s16[2064,256]{1,0:T(8,128)(2,1)S(1)}, u32[]{:S(2)}, u32[]{:S(2)}) collective-permute-start(s16[2064,256]{1,0:T(8,128)(2,1)S(1)} %shard_map.112), channel_id=1, source_target_pairs={{0,8},{1,9},{2,10},{3,11},{4,12},{5,13},{6,14},{7,15},{8,16},{9,17... | collective-permute-start | bytes 3170312 | tf_op jit(solution)/shard_map/ppermute | solution.py:37
  184.9 17.4 %collective-permute-start.24 = (bf16[1024,256]{1,0:T(8,128)(2,1)S(1)}, bf16[1024,256]{1,0:T(8,128)(2,1)S(1)}, u32[]{:S(2)}, u32[]{:S(2)}) collective-permute-start(bf16[1024,256]{1,0:T(8,128)(2,1)S(1)} %slice.46), channel_id=1, source_target_pairs={{0,8},{1,9},{2,10},{3,11},{4,12},{5,13},{6,14},{7,15},{8,16},{9,17... | collective-permute-start | bytes 1572872 | tf_op jit(solution)/shard_map/ppermute | solution.py:37
  185.1 20.9 %collective-permute-start.25 = (bf16[1024,256]{1,0:T(8,128)(2,1)S(1)}, bf16[1024,256]{1,0:T(8,128)(2,1)S(1)}, u32[]{:S(2)}, u32[]{:S(2)}) collective-permute-start(bf16[1024,256]{1,0:T(8,128)(2,1)S(1)} %slice.47), channel_id=1, source_target_pairs={{0,56},{1,57},{2,58},{3,59},{4,60},{5,61},{6,62},{7,63},{8,0},{9,1... | collective-permute-start | bytes 1572872 | tf_op jit(solution)/shard_map/ppermute | solution.py:37
  189.1 8.8 %collective-permute-start.36 = (f32[2,64,672]{2,1,0:T(8,128)S(1)}, f32[2,64,672]{2,1,0:T(8,128)S(1)}, u32[]{:S(2)}, u32[]{:S(2)}) collective-permute-start(f32[2,64,672]{2,1,0:T(8,128)S(1)} %broadcast_multiply_fusion), channel_id=1, source_target_pairs={{0,64},{64,0},{1,65},{65,1},{2,66},{66,2},{3,67},{67,3},{4,68},{68... | collective-permute-start | bytes 1032200 | tf_op jit(solution)/shard_map/ppermute | solution.py:41
  197.2 10.4 %collective-permute-start.29 = (s16[272,256]{1,0:T(8,128)(2,1)S(1)}, s16[272,256]{1,0:T(8,128)(2,1)S(1)}, u32[]{:S(2)}, u32[]{:S(2)}) collective-permute-start(s16[272,256]{1,0:T(8,128)(2,1)S(1)} %get-tuple-element.168), channel_id=1, source_target_pairs={{0,7},{1,0},{2,1},{3,2},{4,3},{5,4},{6,5},{7,6},{8,15},{9,8},{10,9... | collective-permute-start | bytes 417800 | tf_op jit(solution)/shard_map/ppermute | solution.py:37
  197.3 13.9 %collective-permute-start.30 = (s16[272,256]{1,0:T(8,128)(2,1)S(1)}, s16[272,256]{1,0:T(8,128)(2,1)S(1)}, u32[]{:S(2)}, u32[]{:S(2)}) collective-permute-start(s16[272,256]{1,0:T(8,128)(2,1)S(1)} %get-tuple-element.169), channel_id=1, source_target_pairs={{0,6},{1,7},{2,0},{3,1},{4,2},{5,3},{6,4},{7,5},{8,14},{9,15},{10,... | collective-permute-start | bytes 417800 | tf_op jit(solution)/shard_map/ppermute | solution.py:37
  197.9 20.4 %collective-permute-start.31 = (s16[272,256]{1,0:T(8,128)(2,1)S(1)}, s16[272,256]{1,0:T(8,128)(2,1)S(1)}, u32[]{:S(2)}, u32[]{:S(2)}) collective-permute-start(s16[272,256]{1,0:T(8,128)(2,1)S(1)} %get-tuple-element.170), channel_id=1, source_target_pairs={{0,5},{1,6},{2,7},{3,0},{4,1},{5,2},{6,3},{7,4},{8,13},{9,14},{10,... | collective-permute-start | bytes 417800 | tf_op jit(solution)/shard_map/ppermute | solution.py:37
  202.4 15.9 %collective-permute-start.32 = (s16[272,256]{1,0:T(8,128)(2,1)S(1)}, s16[272,256]{1,0:T(8,128)(2,1)S(1)}, u32[]{:S(2)}, u32[]{:S(2)}) collective-permute-start(s16[272,256]{1,0:T(8,128)(2,1)S(1)} %get-tuple-element.171), channel_id=1, source_target_pairs={{0,4},{1,5},{2,6},{3,7},{4,0},{5,1},{6,2},{7,3},{8,12},{9,13},{10,... | collective-permute-start | bytes 417800 | tf_op jit(solution)/shard_map/ppermute | solution.py:37
  206.0 13.1 %collective-permute-start.33 = (s16[272,256]{1,0:T(8,128)(2,1)S(1)}, s16[272,256]{1,0:T(8,128)(2,1)S(1)}, u32[]{:S(2)}, u32[]{:S(2)}) collective-permute-start(s16[272,256]{1,0:T(8,128)(2,1)S(1)} %get-tuple-element.172), channel_id=1, source_target_pairs={{0,3},{1,4},{2,5},{3,6},{4,7},{5,0},{6,1},{7,2},{8,11},{9,12},{10,... | collective-permute-start | bytes 417800 | tf_op jit(solution)/shard_map/ppermute | solution.py:37
  207.5 12.6 %collective-permute-start.34 = (s16[272,256]{1,0:T(8,128)(2,1)S(1)}, s16[272,256]{1,0:T(8,128)(2,1)S(1)}, u32[]{:S(2)}, u32[]{:S(2)}) collective-permute-start(s16[272,256]{1,0:T(8,128)(2,1)S(1)} %get-tuple-element.173), channel_id=1, source_target_pairs={{0,2},{1,3},{2,4},{3,5},{4,6},{5,7},{6,0},{7,1},{8,10},{9,11},{10,... | collective-permute-start | bytes 417800 | tf_op jit(solution)/shard_map/ppermute | solution.py:37
  211.2 10.2 %collective-permute-start.35 = (s16[272,256]{1,0:T(8,128)(2,1)S(1)}, s16[272,256]{1,0:T(8,128)(2,1)S(1)}, u32[]{:S(2)}, u32[]{:S(2)}) collective-permute-start(s16[272,256]{1,0:T(8,128)(2,1)S(1)} %get-tuple-element.174), channel_id=1, source_target_pairs={{0,1},{1,2},{2,3},{3,4},{4,5},{5,6},{6,7},{7,0},{8,9},{9,10},{10,1... | collective-permute-start | bytes 417800 | tf_op jit(solution)/shard_map/ppermute | solution.py:37
  (10 other events, 82.0 us)

commit v2 on v1

--- a/solution.py
+++ b/solution.py
@@ -445,7 +445,6 @@
             live.astype(jnp.float32).reshape(1, token_rows),
         ),
     )
-    hidden = hidden.T
     reduced = jnp.einsum("btr,brk->btk", low_back, chosen_in, preferred_element_type=jnp.float32)
     input_gradient = finish(mine, reduced.reshape(token_rows, width_local), arrived)
 
@@ -460,9 +459,10 @@
         share = table[first : first + each, :blocks_here, None, None]
         return adapter_scale * (share * outer[None]).sum(axis=1)
 
-    grads = of_members(0) + swap(of_members(each))
+    for_other, hidden = tie(of_members(each), hidden)
+    grads = of_members(0) + swap(for_other)
     down_grad = grads[:, :, :width_local].transpose(0, 2, 1)
-    return (hidden, input_gradient, down_grad, grads[:, :, width_local:])
+    return (hidden.T, input_gradient, down_grad, grads[:, :, width_local:])
 
 
 def solution(mesh):

time: 224 us -> 236 us (1.054)
  starting transfers between devices: 70.3 us -> 76.1 us
  waiting for transfers between devices: 92.4 us -> 97.9 us
    ppermute x28, starting transfers between devices: 62.4 us -> 68.2 us  [send(): return lax.ppermute(x, GROUP, ring_pairs(side, step, bulk))]
    ppermute x28, waiting for transfers between devices: 31.6 us -> 37.1 us  [send(): return lax.ppermute(x, GROUP, ring_pairs(side, step, bulk))]
  transfers between devices with their start and end apart: 37 -> 37, of which waited for: 17 -> 15; matrix products, arithmetic and copies ran while one was open for 2% -> 2% of each run, Pallas kernels for 23% -> 23%
where the time goes in v2:
time: 236 us; the launch traced here: 234 us
  waiting for transfers between devices  97.9 us (41%)
  starting transfers between devices  76.1 us (32%)
  Pallas kernels  52.9 us (22%)
  local copies, waits for them, and re-layouts  2.59 us (1%)
    ppermute x28, starting transfers between devices, send(): return lax.ppermute(x, GROUP, ring_pairs(side, step, bulk))  68.2 us
    ppermute x6, waiting for transfers between devices, exchange(): return lax.ppermute(x, GROUP, pairs)  59.4 us
    ppermute x28, waiting for transfers between devices, send(): return lax.ppermute(x, GROUP, ring_pairs(side, step, bulk))  37.1 us
    pallas_call x9, Pallas kernels, reduce_step(): pl.pallas_call(functools.partial(reduce_kernel, parts=len(weights), side=...  29.6 us
    pallas_call x5, Pallas kernels, gather_step(): pl.pallas_call(functools.partial(gather_kernel, parts=len(weights), side=...  21.5 us
    ppermute x6, starting transfers between devices, exchange(): return lax.ppermute(x, GROUP, pairs)  7.47 us
  transfers between devices with their start and end apart: 37, of which 15 were waited for; matrix products, arithmetic and copies ran while one was open for 2% of the time, Pallas kernels for 23%

profile of v2, /device:TPU:518, one launch (start us, length us, event | category | flops | bytes accessed | tf_op | source)
XLA Modules:
  0.0 233.7 jit_solution(5321575823571589253)
XLA Ops:
  4.1 3.2 %collective-permute-done.2 = bf16[256,256]{1,0:T(8,128)(2,1)S(1)} collective-permute-done((bf16[256,256]{1,0:T(8,128)(2,1)}, bf16[256,256]{1,0:T(8,128)(2,1)S(1)}, u32[]{:S(2)}, u32[]{:S(2)}) %collective-permute-start.2) | collective-permute-done | bytes 131104 | tf_op jit(solution)/shard_map/ppermute | solution.py:37
  8.2 18.5 %collective-permute-start.3 = (bf16[512,256]{1,0:T(8,128)(2,1)S(1)}, bf16[512,256]{1,0:T(8,128)(2,1)S(1)}, u32[]{:S(2)}, u32[]{:S(2)}) collective-permute-start(bf16[512,256]{1,0:T(8,128)(2,1)S(1)} %get-tuple-element.186), channel_id=1, source_target_pairs={{0,6},{1,7},{2,0},{3,1},{4,2},{5,3},{6,4},{7,5},{8,14},{9,15},{10,... | collective-permute-start | bytes 786440 | tf_op jit(solution)/shard_map/ppermute | solution.py:37
  30.1 3.3 %collective-permute-done.3 = bf16[512,256]{1,0:T(8,128)(2,1)S(1)} collective-permute-done((bf16[512,256]{1,0:T(8,128)(2,1)S(1)}, bf16[512,256]{1,0:T(8,128)(2,1)S(1)}, u32[]{:S(2)}, u32[]{:S(2)}) %collective-permute-start.3) | collective-permute-done | bytes 262176 | tf_op jit(solution)/shard_map/ppermute | solution.py:37
  33.5 3.4 %collective-permute-done.1 = bf16[512,256]{1,0:T(8,128)(2,1)S(1)} collective-permute-done((bf16[512,256]{1,0:T(8,128)(2,1)S(1)}, bf16[512,256]{1,0:T(8,128)(2,1)S(1)}, u32[]{:S(2)}, u32[]{:S(2)}) %collective-permute-start.1) | collective-permute-done | bytes 262176 | tf_op jit(solution)/shard_map/ppermute | solution.py:37
  45.7 3.2 %collective-permute-start.11 = (s16[1040,256]{1,0:T(8,128)(2,1)S(1)}, s16[1040,256]{1,0:T(8,128)(2,1)S(1)}, u32[]{:S(2)}, u32[]{:S(2)}) collective-permute-start(s16[1040,256]{1,0:T(8,128)(2,1)S(1)} %shard_map.103), channel_id=1, source_target_pairs={{0,56},{1,57},{2,58},{3,59},{4,60},{5,61},{6,62},{7,63},{8,0},{9,1... | collective-permute-start | bytes 1597448 | tf_op jit(solution)/shard_map/ppermute | solution.py:37
  51.4 3.4 %shard_map.105.acc = f32[416,256]{1,0:T(8,128)S(1)} custom-call(f32[416,256]{1,0:T(8,128)S(1)} %broadcast_in_dim.2.acc, bf16[416,8192]{1,0:T(8,128)(2,1)} %bitcast.34, bf16[416,8192]{1,0:T(8,128)(2,1)} %collective-permute-done.4.refs_1_, bf16[2048,256]{1,0:T(8,128)(2,1)S(1)} %constant_dynamic-update-slice_fusion.refs_2_), custom_call_target="tpu_custom_call" | custom-call | flops 436207616 | bytes 2752512 | tf_op jit(solution)/shard_map/pallas_call | solution.py:237
  54.8 10.7 %collective-permute-done.10.refs_2_ = s16[1040,256]{1,0:T(8,128)(2,1)S(1)} collective-permute-done((s16[1040,256]{1,0:T(8,128)(2,1)S(1)}, s16[1040,256]{1,0:T(8,128)(2,1)S(1)}, u32[]{:S(2)}, u32[]{:S(2)}) %collective-permute-start.10) | collective-permute-done | bytes 532512 | tf_op jit(solution)/shard_map/ppermute | solution.py:37
  65.5 3.2 %shard_map.106 = s16[2064,256]{1,0:T(8,128)(2,1)S(1)} custom-call(bf16[256,416]{1,0:T(8,128)(2,1)S(1)} %broadcast_multiply_fusion.1.m.masked, bf16[416,8192]{1,0:T(8,128)(2,1)} %bitcast.35, bf16[416,8192]{1,0:T(8,128)(2,1)} %collective-permute-done.4.refs_1_, s16[1040,256]{1,0:T(8,128)(2,1)S(1)} %collective-permute-done.10.refs_2_), custom_call_target="tpu_custom_call" | custom-call | flops 436207616 | bytes 3801088 | tf_op jit(solution)/shard_map/pallas_call | solution.py:175
  69.5 3.3 %shard_map.107 = s16[2064,256]{1,0:T(8,128)(2,1)S(1)} custom-call(bf16[256,416]{1,0:T(8,128)(2,1)S(1)} %broadcast_multiply_fusion.1.m.masked, bf16[416,8192]{1,0:T(8,128)(2,1)} %bitcast.36, bf16[416,8192]{1,0:T(8,128)(2,1)} %collective-permute-done.4.refs_1_, s16[1040,256]{1,0:T(8,128)(2,1)S(1)} %collective-permute-done.11.refs_2_), custom_call_target="tpu_custom_call" | custom-call | flops 436207616 | bytes 3801088 | tf_op jit(solution)/shard_map/pallas_call | solution.py:175
  75.7 3.2 %collective-permute-start.15 = (bf16[2048,256]{1,0:T(8,128)(2,1)S(1)}, bf16[2048,256]{1,0:T(8,128)(2,1)S(1)}, u32[]{:S(2)}, u32[]{:S(2)}) collective-permute-start(bf16[2048,256]{1,0:T(8,128)(2,1)S(1)} %collective-permute-done.9.refs_3_), channel_id=1, source_target_pairs={{0,56},{1,57},{2,58},{3,59},{4,60},{5,61},{6,62},{7,63},{8,0},{9,1... | collective-permute-start | bytes 3145736 | tf_op jit(solution)/shard_map/ppermute | solution.py:37
  78.9 23.2 %collective-permute-done.7 = f32[256,128]{1,0:T(8,128)S(1)} collective-permute-done((f32[256,128]{1,0:T(8,128)S(1)}, f32[256,128]{1,0:T(8,128)S(1)}, u32[]{:S(2)}, u32[]{:S(2)}) %collective-permute-start.7) | collective-permute-done | bytes 131104 | tf_op jit(solution)/shard_map/ppermute | solution.py:335
  102.2 5.0 %shard_map.108.acc = f32[416,256]{1,0:T(8,128)S(1)} custom-call(f32[416,256]{1,0:T(8,128)S(1)} %shard_map.105.acc, bf16[416,8192]{1,0:T(8,128)(2,1)} %bitcast.37, bf16[416,8192]{1,0:T(8,128)(2,1)} %collective-permute-done.4.refs_1_, bf16[2048,256]{1,0:T(8,128)(2,1)S(1)} %collective-permute-done.8.refs_2_, bf16[2048,256]{1,0:T(8,128)(2,1)S(1)} %collective-permute-done.9.refs_3_), custom_call_target="tpu_custom_call" | custom-call | flops 872415232 | bytes 5505024 | tf_op jit(solution)/shard_map/pallas_call | solution.py:237
  108.6 3.8 %shard_map.109 = s16[2064,256]{1,0:T(8,128)(2,1)S(1)} custom-call(bf16[256,416]{1,0:T(8,128)(2,1)S(1)} %broadcast_multiply_fusion.1.m.masked, bf16[416,8192]{1,0:T(8,128)(2,1)} %bitcast.38, bf16[416,8192]{1,0:T(8,128)(2,1)} %collective-permute-done.4.refs_1_, s16[2064,256]{1,0:T(8,128)(2,1)S(1)} %collective-permute-done.16.refs_2_), custom_call_target="tpu_custom_call" | custom-call | flops 436207616 | bytes 3801088 | tf_op jit(solution)/shard_map/pallas_call | solution.py:175
  112.5 3.8 %shard_map.110 = s16[2064,256]{1,0:T(8,128)(2,1)S(1)} custom-call(bf16[256,416]{1,0:T(8,128)(2,1)S(1)} %broadcast_multiply_fusion.1.m.masked, bf16[416,8192]{1,0:T(8,128)(2,1)} %bitcast.39, bf16[416,8192]{1,0:T(8,128)(2,1)} %collective-permute-done.4.refs_1_, s16[2064,256]{1,0:T(8,128)(2,1)S(1)} %collective-permute-done.17.refs_2_), custom_call_target="tpu_custom_call" | custom-call | flops 436207616 | bytes 3801088 | tf_op jit(solution)/shard_map/pallas_call | solution.py:175
  116.3 3.3 %collective-permute-start.23 = (s16[2064,256]{1,0:T(8,128)(2,1)S(1)}, s16[2064,256]{1,0:T(8,128)(2,1)S(1)}, u32[]{:S(2)}, u32[]{:S(2)}) collective-permute-start(s16[2064,256]{1,0:T(8,128)(2,1)S(1)} %shard_map.110), channel_id=1, source_target_pairs={{0,56},{1,57},{2,58},{3,59},{4,60},{5,61},{6,62},{7,63},{8,0},{9,1... | collective-permute-start | bytes 3170312 | tf_op jit(solution)/shard_map/ppermute | solution.py:37
  119.6 3.2 %collective-permute-start.21 = (bf16[2048,256]{1,0:T(8,128)(2,1)S(1)}, bf16[2048,256]{1,0:T(8,128)(2,1)S(1)}, u32[]{:S(2)}, u32[]{:S(2)}) collective-permute-start(bf16[2048,256]{1,0:T(8,128)(2,1)S(1)} %collective-permute-done.15.refs_3_), channel_id=1, source_target_pairs={{0,56},{1,57},{2,58},{3,59},{4,60},{5,61},{6,62},{7,63},{8,0},{9,1... | collective-permute-start | bytes 3145736 | tf_op jit(solution)/shard_map/ppermute | solution.py:37
  122.8 24.1 %collective-permute-done.13 = f32[256,128]{1,0:T(8,128)S(1)} collective-permute-done((f32[256,128]{1,0:T(8,128)S(1)}, f32[256,128]{1,0:T(8,128)S(1)}, u32[]{:S(2)}, u32[]{:S(2)}) %collective-permute-start.13) | collective-permute-done | bytes 131104 | tf_op jit(solution)/shard_map/ppermute | solution.py:335
  147.1 5.0 %shard_map.111.acc = f32[416,256]{1,0:T(8,128)S(1)} custom-call(f32[416,256]{1,0:T(8,128)S(1)} %shard_map.108.acc, bf16[416,8192]{1,0:T(8,128)(2,1)} %bitcast.40, bf16[416,8192]{1,0:T(8,128)(2,1)} %collective-permute-done.4.refs_1_, bf16[2048,256]{1,0:T(8,128)(2,1)S(1)} %collective-permute-done.14.refs_2_, bf16[2048,256]{1,0:T(8,128)(2,1)S(1)} %collective-permute-done.15.refs_3_), custom_call_target="tpu_custom_call" | custom-call | flops 872415232 | bytes 5505024 | tf_op jit(solution)/shard_map/pallas_call | solution.py:237
  152.1 3.6 %collective-permute-done.18 = f32[256,128]{1,0:T(8,128)S(1)} collective-permute-done((f32[256,128]{1,0:T(8,128)S(1)}, f32[256,128]{1,0:T(8,128)S(1)}, u32[]{:S(2)}, u32[]{:S(2)}) %collective-permute-start.18) | collective-permute-done | bytes 131104 | tf_op jit(solution)/shard_map/ppermute | solution.py:335
  155.7 5.5 %collective-permute-start.19 = (f32[256,128]{1,0:T(8,128)S(1)}, f32[256,128]{1,0:T(8,128)S(1)}, u32[]{:S(2)}, u32[]{:S(2)}) collective-permute-start(f32[256,128]{1,0:T(8,128)S(1)} %add.24), channel_id=1, source_target_pairs={{0,32},{1,33},{2,34},{3,35},{4,36},{5,37},{6,38},{7,39},{8,40},{9,... | collective-permute-start | bytes 393224 | tf_op jit(solution)/shard_map/ppermute | solution.py:335
  161.3 7.3 %collective-permute-done.19 = f32[256,128]{1,0:T(8,128)S(1)} collective-permute-done((f32[256,128]{1,0:T(8,128)S(1)}, f32[256,128]{1,0:T(8,128)S(1)}, u32[]{:S(2)}, u32[]{:S(2)}) %collective-permute-start.19) | collective-permute-done | bytes 131104 | tf_op jit(solution)/shard_map/ppermute | solution.py:335
  168.6 3.8 %shard_map.112 = s16[2064,256]{1,0:T(8,128)(2,1)S(1)} custom-call(bf16[256,416]{1,0:T(8,128)(2,1)S(1)} %broadcast_multiply_fusion.1.m.masked, bf16[416,8192]{1,0:T(8,128)(2,1)} %bitcast.41, bf16[416,8192]{1,0:T(8,128)(2,1)} %collective-permute-done.4.refs_1_, s16[2064,256]{1,0:T(8,128)(2,1)S(1)} %collective-permute-done.22.refs_2_), custom_call_target="tpu_custom_call" | custom-call | flops 436207616 | bytes 3801088 | tf_op jit(solution)/shard_map/pallas_call | solution.py:175
  172.4 3.8 %shard_map.113 = s16[2064,256]{1,0:T(8,128)(2,1)S(1)} custom-call(bf16[256,416]{1,0:T(8,128)(2,1)S(1)} %broadcast_multiply_fusion.1.m.masked, bf16[416,8192]{1,0:T(8,128)(2,1)} %bitcast.42, bf16[416,8192]{1,0:T(8,128)(2,1)} %collective-permute-done.4.refs_1_, s16[2064,256]{1,0:T(8,128)(2,1)S(1)} %collective-permute-done.23.refs_2_), custom_call_target="tpu_custom_call" | custom-call | flops 436207616 | bytes 3801088 | tf_op jit(solution)/shard_map/pallas_call | solution.py:175
  179.9 5.0 %shard_map.114.acc = f32[416,256]{1,0:T(8,128)S(1)} custom-call(f32[416,256]{1,0:T(8,128)S(1)} %shard_map.111.acc, bf16[416,8192]{1,0:T(8,128)(2,1)} %bitcast.43, bf16[416,8192]{1,0:T(8,128)(2,1)} %collective-permute-done.4.refs_1_, bf16[2048,256]{1,0:T(8,128)(2,1)S(1)} %collective-permute-done.20.refs_2_, bf16[2048,256]{1,0:T(8,128)(2,1)S(1)} %collective-permute-done.21.refs_3_), custom_call_target="tpu_custom_call" | custom-call | flops 872415232 | bytes 5505024 | tf_op jit(solution)/shard_map/pallas_call | solution.py:237
  185.1 3.2 %collective-permute-start.26 = (bf16[1024,256]{1,0:T(8,128)(2,1)S(1)}, bf16[1024,256]{1,0:T(8,128)(2,1)S(1)}, u32[]{:S(2)}, u32[]{:S(2)}) collective-permute-start(bf16[1024,256]{1,0:T(8,128)(2,1)S(1)} %slice.50), channel_id=1, source_target_pairs={{0,56},{1,57},{2,58},{3,59},{4,60},{5,61},{6,62},{7,63},{8,0},{9,1... | collective-permute-start | bytes 1572872 | tf_op jit(solution)/shard_map/ppermute | solution.py:37
  189.4 8.4 %collective-permute-done.28.refs_3_ = s16[2064,256]{1,0:T(8,128)(2,1)S(1)} collective-permute-done((s16[2064,256]{1,0:T(8,128)(2,1)S(1)}, s16[2064,256]{1,0:T(8,128)(2,1)S(1)}, u32[]{:S(2)}, u32[]{:S(2)}) %collective-permute-start.28) | collective-permute-done | bytes 1056800 | tf_op jit(solution)/shard_map/ppermute | solution.py:37
  197.8 3.3 %shard_map.116 = (f32[256,256]{1,0:T(8,128)S(1)}, s16[272,256]{1,0:T(8,128)(2,1)S(1)}, s16[272,256]{1,0:T(8,128)(2,1)S(1)}, s16[272,256]{1,0:T(8,128)(2,1)S(1)},...) custom-call(bf16[256,416]{1,0:T(8,128)(2,1)S(1)} %broadcast_multiply, ...), custom_call_target="tpu_custom_call" | custom-call | flops 436207616 | bytes 3801088 | tf_op jit(solution)/shard_map/pallas_call | solution.py:175
  202.9 7.2 %collective-permute-start.31 = (s16[272,256]{1,0:T(8,128)(2,1)S(1)}, s16[272,256]{1,0:T(8,128)(2,1)S(1)}, u32[]{:S(2)}, u32[]{:S(2)}) collective-permute-start(s16[272,256]{1,0:T(8,128)(2,1)S(1)} %get-tuple-element.174), channel_id=1, source_target_pairs={{0,5},{1,6},{2,7},{3,0},{4,1},{5,2},{6,3},{7,4},{8,13},{9,14},{10,... | collective-permute-start | bytes 417800 | tf_op jit(solution)/shard_map/ppermute | solution.py:37
  210.1 3.1 %shard_map.115 = bf16[416,256]{1,0:T(8,128)(2,1)S(1)} custom-call(f32[416,256]{1,0:T(8,128)S(1)} %shard_map.114.acc, bf16[416,8192]{1,0:T(8,128)(2,1)} %bitcast.45, bf16[416,8192]{1,0:T(8,128)(2,1)} %collective-permute-done.4.refs_1_, bf16[1024,256]{1,0:T(8,128)(2,1)S(1)} %collective-permute-done.25.refs_2_, ...), custom_call_target="tpu_custom_call" | custom-call | flops 436207616 | bytes 2752512 | tf_op jit(solution)/shard_map/pallas_call | solution.py:237
  215.0 3.5 %collective-permute-start.33 = (s16[272,256]{1,0:T(8,128)(2,1)S(1)}, s16[272,256]{1,0:T(8,128)(2,1)S(1)}, u32[]{:S(2)}, u32[]{:S(2)}) collective-permute-start(s16[272,256]{1,0:T(8,128)(2,1)S(1)} %get-tuple-element.176), channel_id=1, source_target_pairs={{0,3},{1,4},{2,5},{3,6},{4,7},{5,0},{6,1},{7,2},{8,11},{9,12},{10,... | collective-permute-start | bytes 417800 | tf_op jit(solution)/shard_map/ppermute | solution.py:37
  218.5 3.7 %collective-permute-start.34 = (s16[272,256]{1,0:T(8,128)(2,1)S(1)}, s16[272,256]{1,0:T(8,128)(2,1)S(1)}, u32[]{:S(2)}, u32[]{:S(2)}) collective-permute-start(s16[272,256]{1,0:T(8,128)(2,1)S(1)} %get-tuple-element.177), channel_id=1, source_target_pairs={{0,2},{1,3},{2,4},{3,5},{4,6},{5,7},{6,0},{7,1},{8,10},{9,11},{10,... | collective-permute-start | bytes 417800 | tf_op jit(solution)/shard_map/ppermute | solution.py:37
  224.9 3.8 %collective-permute-done.33.refs_4_ = s16[272,256]{1,0:T(8,128)(2,1)S(1)} collective-permute-done((s16[272,256]{1,0:T(8,128)(2,1)S(1)}, s16[272,256]{1,0:T(8,128)(2,1)S(1)}, u32[]{:S(2)}, u32[]{:S(2)}) %collective-permute-start.33) | collective-permute-done | bytes 139296 | tf_op jit(solution)/shard_map/ppermute | solution.py:37
  (106 shorter events, 40.8 us)
Async XLA Ops:
  0.6 27.1 %collective-permute-start.4 = (bf16[416,8192]{1,0:T(8,128)(2,1)}, bf16[416,8192]{1,0:T(8,128)(2,1)}, u32[]{:S(2)}, u32[]{:S(2)}) collective-permute-start(bf16[416,8192]{1,0:T(8,128)(2,1)} %bitcast.31), channel_id=1, source_target_pairs={{0,64},{64,0},{1,65},{65,1},{2,66},{66,2},{3,67},{67,3},{4,68},{68... | collective-permute-start | bytes 20447240 | tf_op jit(solution)/shard_map/ppermute | solution.py:41
  8.2 25.2 %collective-permute-start.3 = (bf16[512,256]{1,0:T(8,128)(2,1)S(1)}, bf16[512,256]{1,0:T(8,128)(2,1)S(1)}, u32[]{:S(2)}, u32[]{:S(2)}) collective-permute-start(bf16[512,256]{1,0:T(8,128)(2,1)S(1)} %get-tuple-element.186), channel_id=1, source_target_pairs={{0,6},{1,7},{2,0},{3,1},{4,2},{5,3},{6,4},{7,5},{8,14},{9,15},{10,... | collective-permute-start | bytes 786440 | tf_op jit(solution)/shard_map/ppermute | solution.py:37
  26.8 10.1 %collective-permute-start.1 = (bf16[512,256]{1,0:T(8,128)(2,1)S(1)}, bf16[512,256]{1,0:T(8,128)(2,1)S(1)}, u32[]{:S(2)}, u32[]{:S(2)}) collective-permute-start(bf16[512,256]{1,0:T(8,128)(2,1)S(1)} %get-tuple-element.187), channel_id=1, source_target_pairs={{0,2},{1,3},{2,4},{3,5},{4,6},{5,7},{6,0},{7,1},{8,10},{9,11},{10,... | collective-permute-start | bytes 786440 | tf_op jit(solution)/shard_map/ppermute | solution.py:37
  43.5 32.1 %collective-permute-start.9 = (bf16[2048,256]{1,0:T(8,128)(2,1)S(1)}, bf16[2048,256]{1,0:T(8,128)(2,1)S(1)}, u32[]{:S(2)}, u32[]{:S(2)}) collective-permute-start(bf16[2048,256]{1,0:T(8,128)(2,1)S(1)} %constant_dynamic-update-slice_fusion.refs_2_), channel_id=1, source_target_pairs={{0,56},{1,57},{2,58},{3,59},{4,60},{5,61},{6,62},{7,63},{8,0},{9,1... | collective-permute-start | bytes 3145736 | tf_op jit(solution)/shard_map/ppermute | solution.py:37
  43.7 32.0 %collective-permute-start.8 = (bf16[2048,256]{1,0:T(8,128)(2,1)S(1)}, bf16[2048,256]{1,0:T(8,128)(2,1)S(1)}, u32[]{:S(2)}, u32[]{:S(2)}) collective-permute-start(bf16[2048,256]{1,0:T(8,128)(2,1)S(1)} %constant_dynamic-update-slice_fusion.refs_2_), channel_id=1, source_target_pairs={{0,8},{1,9},{2,10},{3,11},{4,12},{5,13},{6,14},{7,15},{8,16},{9,17... | collective-permute-start | bytes 3145736 | tf_op jit(solution)/shard_map/ppermute | solution.py:37
  45.7 19.8 %collective-permute-start.10 = (s16[1040,256]{1,0:T(8,128)(2,1)S(1)}, s16[1040,256]{1,0:T(8,128)(2,1)S(1)}, u32[]{:S(2)}, u32[]{:S(2)}) collective-permute-start(s16[1040,256]{1,0:T(8,128)(2,1)S(1)} %shard_map.102), channel_id=1, source_target_pairs={{0,8},{1,9},{2,10},{3,11},{4,12},{5,13},{6,14},{7,15},{8,16},{9,17... | collective-permute-start | bytes 1597448 | tf_op jit(solution)/shard_map/ppermute | solution.py:37
  45.7 23.9 %collective-permute-start.11 = (s16[1040,256]{1,0:T(8,128)(2,1)S(1)}, s16[1040,256]{1,0:T(8,128)(2,1)S(1)}, u32[]{:S(2)}, u32[]{:S(2)}) collective-permute-start(s16[1040,256]{1,0:T(8,128)(2,1)S(1)} %shard_map.103), channel_id=1, source_target_pairs={{0,56},{1,57},{2,58},{3,59},{4,60},{5,61},{6,62},{7,63},{8,0},{9,1... | collective-permute-start | bytes 1597448 | tf_op jit(solution)/shard_map/ppermute | solution.py:37
  68.7 39.8 %collective-permute-start.16 = (s16[2064,256]{1,0:T(8,128)(2,1)S(1)}, s16[2064,256]{1,0:T(8,128)(2,1)S(1)}, u32[]{:S(2)}, u32[]{:S(2)}) collective-permute-start(s16[2064,256]{1,0:T(8,128)(2,1)S(1)} %shard_map.106), channel_id=1, source_target_pairs={{0,8},{1,9},{2,10},{3,11},{4,12},{5,13},{6,14},{7,15},{8,16},{9,17... | collective-permute-start | bytes 3170312 | tf_op jit(solution)/shard_map/ppermute | solution.py:37
  72.8 39.7 %collective-permute-start.17 = (s16[2064,256]{1,0:T(8,128)(2,1)S(1)}, s16[2064,256]{1,0:T(8,128)(2,1)S(1)}, u32[]{:S(2)}, u32[]{:S(2)}) collective-permute-start(s16[2064,256]{1,0:T(8,128)(2,1)S(1)} %shard_map.107), channel_id=1, source_target_pairs={{0,56},{1,57},{2,58},{3,59},{4,60},{5,61},{6,62},{7,63},{8,0},{9,1... | collective-permute-start | bytes 3170312 | tf_op jit(solution)/shard_map/ppermute | solution.py:37
  75.6 43.9 %collective-permute-start.14 = (bf16[2048,256]{1,0:T(8,128)(2,1)S(1)}, bf16[2048,256]{1,0:T(8,128)(2,1)S(1)}, u32[]{:S(2)}, u32[]{:S(2)}) collective-permute-start(bf16[2048,256]{1,0:T(8,128)(2,1)S(1)} %collective-permute-done.8.refs_2_), channel_id=1, source_target_pairs={{0,8},{1,9},{2,10},{3,11},{4,12},{5,13},{6,14},{7,15},{8,16},{9,17... | collective-permute-start | bytes 3145736 | tf_op jit(solution)/shard_map/ppermute | solution.py:37
  75.7 43.9 %collective-permute-start.15 = (bf16[2048,256]{1,0:T(8,128)(2,1)S(1)}, bf16[2048,256]{1,0:T(8,128)(2,1)S(1)}, u32[]{:S(2)}, u32[]{:S(2)}) collective-permute-start(bf16[2048,256]{1,0:T(8,128)(2,1)S(1)} %collective-permute-done.9.refs_3_), channel_id=1, source_target_pairs={{0,56},{1,57},{2,58},{3,59},{4,60},{5,61},{6,62},{7,63},{8,0},{9,1... | collective-permute-start | bytes 3145736 | tf_op jit(solution)/shard_map/ppermute | solution.py:37
  78.9 23.2 %collective-permute-start.7 = (f32[256,128]{1,0:T(8,128)S(1)}, f32[256,128]{1,0:T(8,128)S(1)}, u32[]{:S(2)}, u32[]{:S(2)}) collective-permute-start(f32[256,128]{1,0:T(8,128)S(1)} %get-tuple-element.100), channel_id=1, source_target_pairs={{0,8},{1,9},{2,10},{3,11},{4,12},{5,13},{6,14},{7,15},{8,0},{9,1},... | collective-permute-start | bytes 393224 | tf_op jit(solution)/shard_map/ppermute | solution.py:335
  112.4 56.2 %collective-permute-start.22 = (s16[2064,256]{1,0:T(8,128)(2,1)S(1)}, s16[2064,256]{1,0:T(8,128)(2,1)S(1)}, u32[]{:S(2)}, u32[]{:S(2)}) collective-permute-start(s16[2064,256]{1,0:T(8,128)(2,1)S(1)} %shard_map.109), channel_id=1, source_target_pairs={{0,8},{1,9},{2,10},{3,11},{4,12},{5,13},{6,14},{7,15},{8,16},{9,17... | collective-permute-start | bytes 3170312 | tf_op jit(solution)/shard_map/ppermute | solution.py:37
  116.3 56.1 %collective-permute-start.23 = (s16[2064,256]{1,0:T(8,128)(2,1)S(1)}, s16[2064,256]{1,0:T(8,128)(2,1)S(1)}, u32[]{:S(2)}, u32[]{:S(2)}) collective-permute-start(s16[2064,256]{1,0:T(8,128)(2,1)S(1)} %shard_map.110), channel_id=1, source_target_pairs={{0,56},{1,57},{2,58},{3,59},{4,60},{5,61},{6,62},{7,63},{8,0},{9,1... | collective-permute-start | bytes 3170312 | tf_op jit(solution)/shard_map/ppermute | solution.py:37
  119.6 56.6 %collective-permute-start.20 = (bf16[2048,256]{1,0:T(8,128)(2,1)S(1)}, bf16[2048,256]{1,0:T(8,128)(2,1)S(1)}, u32[]{:S(2)}, u32[]{:S(2)}) collective-permute-start(bf16[2048,256]{1,0:T(8,128)(2,1)S(1)} %collective-permute-done.14.refs_2_), channel_id=1, source_target_pairs={{0,8},{1,9},{2,10},{3,11},{4,12},{5,13},{6,14},{7,15},{8,16},{9,17... | collective-permute-start | bytes 3145736 | tf_op jit(solution)/shard_map/ppermute | solution.py:37
  119.6 56.6 %collective-permute-start.21 = (bf16[2048,256]{1,0:T(8,128)(2,1)S(1)}, bf16[2048,256]{1,0:T(8,128)(2,1)S(1)}, u32[]{:S(2)}, u32[]{:S(2)}) collective-permute-start(bf16[2048,256]{1,0:T(8,128)(2,1)S(1)} %collective-permute-done.15.refs_3_), channel_id=1, source_target_pairs={{0,56},{1,57},{2,58},{3,59},{4,60},{5,61},{6,62},{7,63},{8,0},{9,1... | collective-permute-start | bytes 3145736 | tf_op jit(solution)/shard_map/ppermute | solution.py:37
  122.8 24.1 %collective-permute-start.13 = (f32[256,128]{1,0:T(8,128)S(1)}, f32[256,128]{1,0:T(8,128)S(1)}, u32[]{:S(2)}, u32[]{:S(2)}) collective-permute-start(f32[256,128]{1,0:T(8,128)S(1)} %add.22), channel_id=1, source_target_pairs={{0,16},{1,17},{2,18},{3,19},{4,20},{5,21},{6,22},{7,23},{8,24},{9,... | collective-permute-start | bytes 393224 | tf_op jit(solution)/shard_map/ppermute | solution.py:335
  146.9 8.8 %collective-permute-start.18 = (f32[256,128]{1,0:T(8,128)S(1)}, f32[256,128]{1,0:T(8,128)S(1)}, u32[]{:S(2)}, u32[]{:S(2)}) collective-permute-start(f32[256,128]{1,0:T(8,128)S(1)} %add.23), channel_id=1, source_target_pairs={{0,2},{1,3},{2,0},{3,1},{4,6},{5,7},{6,4},{7,5},{8,10},{9,11},{10,... | collective-permute-start | bytes 393224 | tf_op jit(solution)/shard_map/ppermute | solution.py:335
  155.7 12.8 %collective-permute-start.19 = (f32[256,128]{1,0:T(8,128)S(1)}, f32[256,128]{1,0:T(8,128)S(1)}, u32[]{:S(2)}, u32[]{:S(2)}) collective-permute-start(f32[256,128]{1,0:T(8,128)S(1)} %add.24), channel_id=1, source_target_pairs={{0,32},{1,33},{2,34},{3,35},{4,36},{5,37},{6,38},{7,39},{8,40},{9,... | collective-permute-start | bytes 393224 | tf_op jit(solution)/shard_map/ppermute | solution.py:335
  176.2 12.1 %collective-permute-start.24 = (f32[256,128]{1,0:T(8,128)S(1)}, f32[256,128]{1,0:T(8,128)S(1)}, u32[]{:S(2)}, u32[]{:S(2)}) collective-permute-start(f32[256,128]{1,0:T(8,128)S(1)} %add.25), channel_id=1, source_target_pairs={{0,4},{1,5},{2,6},{3,7},{4,0},{5,1},{6,2},{7,3},{8,12},{9,13},{10,... | collective-permute-start | bytes 393224 | tf_op jit(solution)/shard_map/ppermute | solution.py:335
  177.8 20.0 %collective-permute-start.28 = (s16[2064,256]{1,0:T(8,128)(2,1)S(1)}, s16[2064,256]{1,0:T(8,128)(2,1)S(1)}, u32[]{:S(2)}, u32[]{:S(2)}) collective-permute-start(s16[2064,256]{1,0:T(8,128)(2,1)S(1)} %shard_map.113), channel_id=1, source_target_pairs={{0,56},{1,57},{2,58},{3,59},{4,60},{5,61},{6,62},{7,63},{8,0},{9,1... | collective-permute-start | bytes 3170312 | tf_op jit(solution)/shard_map/ppermute | solution.py:37
  177.8 20.0 %collective-permute-start.27 = (s16[2064,256]{1,0:T(8,128)(2,1)S(1)}, s16[2064,256]{1,0:T(8,128)(2,1)S(1)}, u32[]{:S(2)}, u32[]{:S(2)}) collective-permute-start(s16[2064,256]{1,0:T(8,128)(2,1)S(1)} %shard_map.112), channel_id=1, source_target_pairs={{0,8},{1,9},{2,10},{3,11},{4,12},{5,13},{6,14},{7,15},{8,16},{9,17... | collective-permute-start | bytes 3170312 | tf_op jit(solution)/shard_map/ppermute | solution.py:37
  184.9 25.1 %collective-permute-start.25 = (bf16[1024,256]{1,0:T(8,128)(2,1)S(1)}, bf16[1024,256]{1,0:T(8,128)(2,1)S(1)}, u32[]{:S(2)}, u32[]{:S(2)}) collective-permute-start(bf16[1024,256]{1,0:T(8,128)(2,1)S(1)} %slice.49), channel_id=1, source_target_pairs={{0,8},{1,9},{2,10},{3,11},{4,12},{5,13},{6,14},{7,15},{8,16},{9,17... | collective-permute-start | bytes 1572872 | tf_op jit(solution)/shard_map/ppermute | solution.py:37
  185.1 25.0 %collective-permute-start.26 = (bf16[1024,256]{1,0:T(8,128)(2,1)S(1)}, bf16[1024,256]{1,0:T(8,128)(2,1)S(1)}, u32[]{:S(2)}, u32[]{:S(2)}) collective-permute-start(bf16[1024,256]{1,0:T(8,128)(2,1)S(1)} %slice.50), channel_id=1, source_target_pairs={{0,56},{1,57},{2,58},{3,59},{4,60},{5,61},{6,62},{7,63},{8,0},{9,1... | collective-permute-start | bytes 1572872 | tf_op jit(solution)/shard_map/ppermute | solution.py:37
  201.1 13.9 %collective-permute-start.29 = (s16[272,256]{1,0:T(8,128)(2,1)S(1)}, s16[272,256]{1,0:T(8,128)(2,1)S(1)}, u32[]{:S(2)}, u32[]{:S(2)}) collective-permute-start(s16[272,256]{1,0:T(8,128)(2,1)S(1)} %get-tuple-element.172), channel_id=1, source_target_pairs={{0,7},{1,0},{2,1},{3,2},{4,3},{5,4},{6,5},{7,6},{8,15},{9,8},{10,9... | collective-permute-start | bytes 417800 | tf_op jit(solution)/shard_map/ppermute | solution.py:37
  202.9 15.6 %collective-permute-start.30 = (s16[272,256]{1,0:T(8,128)(2,1)S(1)}, s16[272,256]{1,0:T(8,128)(2,1)S(1)}, u32[]{:S(2)}, u32[]{:S(2)}) collective-permute-start(s16[272,256]{1,0:T(8,128)(2,1)S(1)} %get-tuple-element.173), channel_id=1, source_target_pairs={{0,6},{1,7},{2,0},{3,1},{4,2},{5,3},{6,4},{7,5},{8,14},{9,15},{10,... | collective-permute-start | bytes 417800 | tf_op jit(solution)/shard_map/ppermute | solution.py:37
  202.9 19.3 %collective-permute-start.31 = (s16[272,256]{1,0:T(8,128)(2,1)S(1)}, s16[272,256]{1,0:T(8,128)(2,1)S(1)}, u32[]{:S(2)}, u32[]{:S(2)}) collective-permute-start(s16[272,256]{1,0:T(8,128)(2,1)S(1)} %get-tuple-element.174), channel_id=1, source_target_pairs={{0,5},{1,6},{2,7},{3,0},{4,1},{5,2},{6,3},{7,4},{8,13},{9,14},{10,... | collective-permute-start | bytes 417800 | tf_op jit(solution)/shard_map/ppermute | solution.py:37
  213.1 19.1 %collective-permute-start.36 = (f32[2,64,672]{2,1,0:T(8,128)S(1)}, f32[2,64,672]{2,1,0:T(8,128)S(1)}, u32[]{:S(2)}, u32[]{:S(2)}) collective-permute-start(f32[2,64,672]{2,1,0:T(8,128)S(1)} %broadcast_multiply_fusion), channel_id=1, source_target_pairs={{0,64},{64,0},{1,65},{65,1},{2,66},{66,2},{3,67},{67,3},{4,68},{68... | collective-permute-start | bytes 1032200 | tf_op jit(solution)/shard_map/ppermute | solution.py:41
  213.3 11.6 %collective-permute-start.32 = (s16[272,256]{1,0:T(8,128)(2,1)S(1)}, s16[272,256]{1,0:T(8,128)(2,1)S(1)}, u32[]{:S(2)}, u32[]{:S(2)}) collective-permute-start(s16[272,256]{1,0:T(8,128)(2,1)S(1)} %get-tuple-element.175), channel_id=1, source_target_pairs={{0,4},{1,5},{2,6},{3,7},{4,0},{5,1},{6,2},{7,3},{8,12},{9,13},{10,... | collective-permute-start | bytes 417800 | tf_op jit(solution)/shard_map/ppermute | solution.py:37
  215.0 13.7 %collective-permute-start.33 = (s16[272,256]{1,0:T(8,128)(2,1)S(1)}, s16[272,256]{1,0:T(8,128)(2,1)S(1)}, u32[]{:S(2)}, u32[]{:S(2)}) collective-permute-start(s16[272,256]{1,0:T(8,128)(2,1)S(1)} %get-tuple-element.176), channel_id=1, source_target_pairs={{0,3},{1,4},{2,5},{3,6},{4,7},{5,0},{6,1},{7,2},{8,11},{9,12},{10,... | collective-permute-start | bytes 417800 | tf_op jit(solution)/shard_map/ppermute | solution.py:37
  218.5 11.5 %collective-permute-start.34 = (s16[272,256]{1,0:T(8,128)(2,1)S(1)}, s16[272,256]{1,0:T(8,128)(2,1)S(1)}, u32[]{:S(2)}, u32[]{:S(2)}) collective-permute-start(s16[272,256]{1,0:T(8,128)(2,1)S(1)} %get-tuple-element.177), channel_id=1, source_target_pairs={{0,2},{1,3},{2,4},{3,5},{4,6},{5,7},{6,0},{7,1},{8,10},{9,11},{10,... | collective-permute-start | bytes 417800 | tf_op jit(solution)/shard_map/ppermute | solution.py:37
  222.2 9.2 %collective-permute-start.35 = (s16[272,256]{1,0:T(8,128)(2,1)S(1)}, s16[272,256]{1,0:T(8,128)(2,1)S(1)}, u32[]{:S(2)}, u32[]{:S(2)}) collective-permute-start(s16[272,256]{1,0:T(8,128)(2,1)S(1)} %get-tuple-element.178), channel_id=1, source_target_pairs={{0,1},{1,2},{2,3},{3,4},{4,5},{5,6},{6,7},{7,0},{8,9},{9,10},{10,1... | collective-permute-start | bytes 417800 | tf_op jit(solution)/shard_map/ppermute | solution.py:37
  (10 other events, 82.0 us)
